TPU v7x, 512 devices: a whole 4x4x16 slice. The times are simulated.
512 devices in a mesh: dp: 32 (over z_lo, x), mp: 16 (over y, z_hi, core).
Axes of the slice: x: 4, y: 4, z: 16 (z_hi: 2, z_lo: 8; z = z_hi * 8 + z_lo), core: 2. Of those that a mesh axis runs over, the one named last changes fastest.
Arguments:
- hidden: bfloat16 [512, 4096], P('dp'), may hold values from -6 to 6
- wq_direct: bfloat16 [4096, 2048], P(None, 'mp'), may hold values from -0.09375 to 0.09375
- wkv_direct: bfloat16 [2, 4096, 2048], P(None, None, 'mp'), may hold values from -0.09375 to 0.09375
- wo_direct: bfloat16 [2048, 4096], P(None, 'mp'), may hold values from -0.125 to 0.125
- kv_cache: bfloat16 [2, 512, 32, 2048], P(None, 'dp', None, 'mp'), may hold values from -6 to 6
- parent: int32 [512], P('dp'), may hold values from 0 to 15
- lengths: int32 [512], P('dp'), may hold values from 1 to 32
- cand_embed: bfloat16 [512, 32, 4096], P('dp', None, 'mp'), may hold values from -6 to 6
- source: bfloat16 [32, 8, 4096], P('dp', None, 'mp'), may hold values from -6 to 6
- enc_qkv: bfloat16 [3, 4096, 2048], P(None, 'dp', 'mp'), may hold values from -0.09375 to 0.09375
- enc_out: bfloat16 [2048, 4096], P('dp', 'mp'), may hold values from -0.125 to 0.125
- cross_q: bfloat16 [4096, 2048], P('dp', 'mp'), may hold values from -0.09375 to 0.09375
- cross_kv: bfloat16 [2, 4096, 2048], P(None, 'dp', 'mp'), may hold values from -0.09375 to 0.09375
- cross_out: bfloat16 [2048, 4096], P('dp', 'mp'), may hold values from -0.125 to 0.125
- w_direct: bfloat16 [4096], P('mp'), may hold values from -0.09375 to 0.09375
- w_channel: bfloat16 [4096], P('mp'), may hold values from -0.09375 to 0.09375
- target_shard: int32 [512], P('dp'), may hold values from 0 to 31, as said below
Outputs:
- direct_state: bfloat16 [512, 4096], P('dp', 'mp')
- rerank_score: float32 [512], P('dp')
- channel_score: float32 [512], P('dp')
Inputs may be any that keep to these rules, and one draw needn't show every extreme that they name: `target_shard`: every shard receives exactly one candidate of each beam index; a device sends exactly 1 of its candidates to each shard that it sends to.
All inputs are finite; a program needn't handle non-finite values.
Results may differ from a plain program's by a relative error of at most 0.0075.
Values may be sent and summed in bfloat16 or wider, within the bound.
A program may use at most 128 MiB of HBM per device.

v0:
```python
import math

import jax
import jax.numpy as jnp
from jax import lax
from jax.sharding import Mesh
from jax.sharding import PartitionSpec as P

D = 4096
HD = 64
MP = ("mp_0", "mp_1", "mp_2")


EPSILON = 1e-06


def sent_to_all(array, axis):
    copies = jnp.broadcast_to(array, (lax.axis_size(axis), *array.shape))
    return lax.all_to_all(copies, axis, split_axis=0, concat_axis=0, tiled=True)


def joined_along(tiles, dim):
    shape = list(tiles.shape[1:])
    shape[dim] *= tiles.shape[0]
    return jnp.moveaxis(tiles, 0, dim).reshape(shape)


def gather_axes(array, axes, dim):
    far, near = axes
    initial = sent_to_all(array, far)
    tiles = jnp.swapaxes(sent_to_all(initial, near), 0, 1)
    return joined_along(tiles.reshape(-1, *array.shape), dim)


def taken_together(array, axis):
    everything = sent_to_all(array, axis)
    return jnp.sum(everything, axis=0)


def gather_packed(arrays, axis, dims):
    line = jnp.concatenate([a.reshape(-1) for a in arrays])
    lines, at, done = (lax.all_gather(line, axis), 0, [])
    for a, dim in zip(arrays, dims):
        tiles = lines[:, at : at + a.size].reshape(-1, *a.shape)
        done.append(joined_along(tiles, dim))
        at += a.size
    return tuple(done)


def side_by_side(arrays, axis, split_dim, concat_dim, along):
    widths = [math.prod(a.shape[along:]) for a in arrays]
    both = jnp.concatenate(
        [a.reshape(*a.shape[:along], w) for a, w in zip(arrays, widths)], axis=along
    )
    whole = lax.all_to_all(both, axis, split_axis=split_dim, concat_axis=concat_dim, tiled=True)
    tiles = jnp.split(whole, [sum(widths[:k]) for k in range(1, len(widths))], axis=along)
    return tuple((b.reshape(*whole.shape[:along], *a.shape[along:]) for a, b in zip(arrays, tiles)))


def attend(queries, keys, values, valid):
    group_n, query_n, columns = queries.shape
    key_n = keys.shape[1]
    head_n = columns // HD
    query_heads = queries.reshape(group_n, query_n, head_n, HD)
    key_heads = keys.reshape(group_n, key_n, head_n, HD)
    value_heads = values.reshape(group_n, key_n, head_n, HD)
    scores = jnp.einsum(
        "bqhd,bkhd->bhqk", query_heads, key_heads, preferred_element_type=jnp.float32
    ) / math.sqrt(HD)
    scores = jnp.where(valid[:, None, None, :], scores, -1e30)
    weights = jax.nn.softmax(scores, axis=-1).astype(jnp.bfloat16)
    context = jnp.einsum(
        "bhqk,bkhd->bqhd", weights, value_heads, preferred_element_type=jnp.float32
    )
    return context.astype(jnp.bfloat16).reshape(group_n, query_n, columns)


def project(inputs, matrices):
    segment = gather_axes(inputs, (("mp_0", "mp_1"), "mp_2"), 1)
    return tuple(
        (jnp.dot(segment, matrix, preferred_element_type=jnp.float32) for matrix in matrices)
    )


def row_sums(parts):
    return jax.tree.map(lambda part: taken_together(part, MP), parts)


def shards(
    hidden,
    wq_direct,
    wkv_direct,
    wo_direct,
    kv_cache,
    parent,
    lengths,
    cand_embed,
    source,
    enc_qkv,
    enc_out,
    cross_q,
    cross_kv,
    cross_out,
    w_direct,
    w_channel,
    target_shard,
):
    enc_full, out_full, query_full, memory_full, cross_full = gather_packed(
        (enc_qkv, enc_out, cross_q, cross_kv, cross_out), "dp", (1, 0, 0, 1, 0)
    )
    beam_n = hidden.shape[0]
    local_width = wo_direct.shape[1]
    cache_len = kv_cache.shape[2]
    beam_index = jnp.arange(beam_n, dtype=jnp.int32)
    positions = jnp.arange(cache_len, dtype=jnp.int32)
    own_start = lax.axis_index(MP) * local_width
    hidden_share = lax.dynamic_slice_in_dim(hidden, own_start, local_width, 1).astype(jnp.float32)
    query_new = jnp.dot(hidden, wq_direct, preferred_element_type=jnp.float32).astype(jnp.bfloat16)
    key_new = jnp.dot(hidden, wkv_direct[0], preferred_element_type=jnp.float32).astype(
        jnp.bfloat16
    )
    value_new = jnp.dot(hidden, wkv_direct[1], preferred_element_type=jnp.float32).astype(
        jnp.bfloat16
    )
    all_keys = jnp.concatenate([kv_cache[0][parent], key_new[:, None]], axis=1)
    all_values = jnp.concatenate([kv_cache[1][parent], value_new[:, None]], axis=1)
    cache_valid = jnp.concatenate(
        [positions[None, :] < lengths[:, None], jnp.ones((beam_n, 1), dtype=bool)], axis=1
    )
    context = attend(query_new[:, None], all_keys, all_values, cache_valid)[:, 0]
    (update,) = project(context, (wo_direct,))
    new_state = hidden_share + update
    squares, direct_dot = row_sums(
        (
            jnp.sum(new_state * new_state, axis=1),
            jnp.sum(new_state * w_direct.astype(jnp.float32), axis=1),
        )
    )
    direct_score = direct_dot / jnp.sqrt(squares / D + EPSILON)
    peer_count = lax.axis_size("dp")
    per_peer = max(1, beam_n // peer_count)
    slots_total = peer_count * per_peer
    same_shard = target_shard[:, None] == target_shard[None, :]
    earlier = beam_index[None, :] < beam_index[:, None]
    rank_within = jnp.sum(same_shard & earlier, axis=1)
    send_slot = target_shard * per_peer + rank_within
    tokens = cand_embed[parent]
    own_source = source[0]
    src_len = own_source.shape[0]
    send_tokens = (
        jnp.zeros((slots_total,) + tokens.shape[1:], jnp.bfloat16).at[send_slot].set(tokens)
    )
    send_source = (
        jnp.zeros((slots_total, src_len, local_width), jnp.bfloat16)
        .at[send_slot]
        .set(jnp.broadcast_to(own_source[None], (beam_n, src_len, local_width)))
    )
    labels = jnp.stack([beam_index, lengths], axis=1).astype(jnp.bfloat16)
    send_labels = jnp.full((slots_total, 2), -1.0, jnp.bfloat16).at[send_slot].set(labels)
    got_tokens, got_source, got_labels = side_by_side(
        (send_tokens, send_source, send_labels), "dp", 0, 0, 1
    )
    beam_match = got_labels[:, 0].astype(jnp.int32)[None, :] == beam_index[:, None]
    arrival = jnp.argmax(beam_match, axis=1)
    cand_tokens = got_tokens[arrival]
    cand_source = got_source[arrival]
    cand_len = got_labels[arrival, 1].astype(jnp.int32)
    token_rows = cand_tokens.reshape(beam_n * cache_len, local_width)
    enc_queries, enc_keys, enc_values = project(token_rows, (enc_full[0], enc_full[1], enc_full[2]))
    enc_queries = enc_queries.astype(jnp.bfloat16).reshape(beam_n, cache_len, -1)
    enc_keys = enc_keys.astype(jnp.bfloat16).reshape(beam_n, cache_len, -1)
    enc_values = enc_values.astype(jnp.bfloat16).reshape(beam_n, cache_len, -1)
    key_valid = positions[None, :] < cand_len[:, None]
    enc_context = attend(enc_queries, enc_keys, enc_values, key_valid).reshape(
        beam_n * cache_len, -1
    )
    (enc_update,) = project(enc_context, (out_full,))
    summed = token_rows.astype(jnp.float32) + enc_update
    (enc_squares,) = row_sums((jnp.sum(summed * summed, axis=1),))
    memory = (summed / jnp.sqrt(enc_squares / D + EPSILON)[:, None]).astype(jnp.bfloat16)
    cross_keys, cross_values = project(memory, (memory_full[0], memory_full[1]))
    cross_keys = cross_keys.astype(jnp.bfloat16).reshape(beam_n, cache_len, -1)
    cross_values = cross_values.astype(jnp.bfloat16).reshape(beam_n, cache_len, -1)
    source_rows = cand_source.reshape(beam_n * src_len, local_width)
    (cross_queries,) = project(source_rows, (query_full,))
    cross_queries = cross_queries.astype(jnp.bfloat16).reshape(beam_n, src_len, -1)
    cross_context = attend(cross_queries, cross_keys, cross_values, key_valid).reshape(
        beam_n * src_len, -1
    )
    (cross_update,) = project(cross_context, (cross_full,))
    decoded = source_rows.astype(jnp.float32) + cross_update
    dec_squares, dec_dot = row_sums(
        (
            jnp.sum(decoded * decoded, axis=1),
            jnp.sum(decoded * w_channel.astype(jnp.float32), axis=1),
        )
    )
    position_score = (dec_dot / jnp.sqrt(dec_squares / D + EPSILON)).reshape(beam_n, src_len)
    channel_score = jnp.mean(position_score, axis=1)
    send_back = jnp.zeros((slots_total,), jnp.float32).at[arrival].set(channel_score)
    returned = lax.all_to_all(send_back, "dp", split_axis=0, concat_axis=0, tiled=True)
    rerank_score = direct_score + returned[send_slot]
    return (new_state.astype(jnp.bfloat16), rerank_score, channel_score)


def solution(mesh):
    split = Mesh(mesh.devices.reshape(mesh.shape["dp"], 4, 2, 2), ("dp", "mp_0", "mp_1", "mp_2"))
    in_specs = (
        P("dp", None),
        P(None, MP),
        P(None, None, MP),
        P(None, MP),
        P(None, "dp", None, MP),
        P("dp"),
        P("dp"),
        P("dp", None, MP),
        P("dp", None, MP),
        P(None, "dp", MP),
        P("dp", MP),
        P("dp", MP),
        P(None, "dp", MP),
        P("dp", MP),
        P(MP),
        P(MP),
        P("dp"),
    )
    out_specs = (P("dp", MP), P("dp"), P("dp"))
    return jax.shard_map(
        shards, mesh=split, in_specs=in_specs, out_specs=out_specs, check_vma=False
    )
```

profile of v0, /device:TPU:1, one launch (start us, length us, event | category | flops | bytes accessed | tf_op | source)
XLA Modules:
  0.0 738.7 jit_solution(10287506021076449169)
XLA Ops:
  22.8 70.6 %all_to_all.114 = bf16[32,2,5121]{2,1,0:T(2,128)(2,1)S(1)} all-to-all(bf16[32,2,5121]{2,1,0:T(2,128)(2,1)S(1)} %reshape.348), channel_id=1, replica_groups=mesh['dp'=32,'mp_0'=4,'mp_1'=2,'mp_2'=2] {'dp'}, dimensions={0} | all-to-all | bytes 1310976 | tf_op jit(solution)/shard_map/all_to_all | solution.py:55
  111.8 46.6 %all-to-all-done.5 = bf16[8,512,256]{2,1,0:T(8,128)(2,1)S(1)} async-done(((bf16[8,512,256]{2,1,0:T(8,128)(2,1)}), bf16[8,512,256]{2,1,0:T(8,128)(2,1)S(1)}, u32[]{:S(2)}, u32[]{:S(2)}) %all-to-all-start.5) | async-done | bytes 2097184 | tf_op jit(solution)/shard_map/all_to_all | solution.py:19
  158.8 15.3 %all_to_all.115 = bf16[2,8,512,256]{3,2,1,0:T(8,128)(2,1)S(1)} all-to-all(bf16[2,8,512,256]{3,2,1,0:T(8,128)(2,1)S(1)} %broadcast_in_dim.167), channel_id=1, replica_groups=mesh['dp'=32,'mp_0'=4,'mp_1'=2,'mp_2'=2] {'mp_2'}, dimensions={0} | all-to-all | bytes 8388608 | tf_op jit(solution)/shard_map/all_to_all | solution.py:19
  176.3 6.4 copy.161
  182.7 112.7 %all-gather.3.cloned.1.call-done = bf16[4194304]{0:T(1024)(128)(2,1)} async-done(((bf16[131072]{0:T(1024)(128)(2,1)}), bf16[4194304]{0:T(1024)(128)(2,1)}) %all-gather.3.cloned.1.call-update) | async-done | bytes 8388624 | tf_op jit(solution)/shard_map/all_gather | solution.py:42
  295.5 8.7 %reshape.318 = bf16[32,131072]{1,0:T(8,128)(2,1)} reshape(bf16[4194304]{0:T(1024)(128)(2,1)} %all-gather.3.cloned.1.call-done) | data formatting | bytes 16777216 | tf_op jit(solution)/shard_map/all_gather | solution.py:42
  315.9 22.1 %all-to-all-start.7 = ((bf16[8,512,128]{2,1,0:T(8,128)(2,1)}), bf16[8,512,128]{2,1,0:T(8,128)(2,1)S(1)}, u32[]{:S(2)}, u32[]{:S(2)}) async-start(bf16[8,512,128]{2,1,0:T(8,128)(2,1)} %broadcast_in_dim.170), calls=%async_computation.7 | async-start | bytes 2097152 | tf_op jit(solution)/shard_map/all_to_all | solution.py:19
  340.8 19.1 %all-to-all-done.7 = bf16[8,512,128]{2,1,0:T(8,128)(2,1)S(1)} async-done(((bf16[8,512,128]{2,1,0:T(8,128)(2,1)}), bf16[8,512,128]{2,1,0:T(8,128)(2,1)S(1)}, u32[]{:S(2)}, u32[]{:S(2)}) %all-to-all-start.7) | async-done | bytes 1048608 | tf_op jit(solution)/shard_map/all_to_all | solution.py:19
  360.3 40.2 %all_to_all.116 = bf16[2,8,512,128]{3,2,1,0:T(8,128)(2,1)S(1)} all-to-all(bf16[2,8,512,128]{3,2,1,0:T(8,128)(2,1)S(1)} %broadcast_in_dim.171), channel_id=1, replica_groups=mesh['dp'=32,'mp_0'=4,'mp_1'=2,'mp_2'=2] {'mp_2'}, dimensions={0} | all-to-all | bytes 4194304 | tf_op jit(solution)/shard_map/all_to_all | solution.py:19
  401.3 11.3 %all-to-all-start.12 = ((bf16[8,128,256]{2,1,0:T(8,128)(2,1)}), bf16[8,128,256]{2,1,0:T(8,128)(2,1)}, u32[]{:S(2)}, u32[]{:S(2)}) async-start(bf16[8,128,256]{2,1,0:T(8,128)(2,1)} %broadcast_in_dim.176), calls=%async_computation.12 | async-start | bytes 1048576 | tf_op jit(solution)/shard_map/all_to_all | solution.py:19
  430.8 47.3 %all_to_all.117 = f32[16,1,512]{2,1,0:T(1,128)S(1)} all-to-all(f32[16,1,512]{2,1,0:T(1,128)S(1)} %broadcast_in_dim.172), channel_id=1, replica_groups=mesh['dp'=32,'mp_0'=4,'mp_1'=2,'mp_2'=2] {'mp_0','mp_1','mp_2'}, dimensions={0} | all-to-all | bytes 65536 | tf_op jit(solution)/shard_map/all_to_all | solution.py:19
  487.8 11.8 %all-to-all-start.10 = ((bf16[8,512,256]{2,1,0:T(8,128)(2,1)}), bf16[8,512,256]{2,1,0:T(8,128)(2,1)S(1)}, u32[]{:S(2)}, u32[]{:S(2)}) async-start(bf16[8,512,256]{2,1,0:T(8,128)(2,1)} %broadcast_in_dim.173), calls=%async_computation.10 | async-start | bytes 4194304 | tf_op jit(solution)/shard_map/all_to_all | solution.py:19
  535.4 9.4 %all_to_all.118 = bf16[2,8,512,256]{3,2,1,0:T(8,128)(2,1)} all-to-all(bf16[2,8,512,256]{3,2,1,0:T(8,128)(2,1)S(1)} %broadcast_in_dim.174), channel_id=1, replica_groups=mesh['dp'=32,'mp_0'=4,'mp_1'=2,'mp_2'=2] {'mp_2'}, dimensions={0} | all-to-all | bytes 8388608 | tf_op jit(solution)/shard_map/all_to_all | solution.py:19
  545.4 11.3 %all-to-all-start = ((bf16[8,16,128]{2,1,0:T(8,128)(2,1)}), bf16[8,16,128]{2,1,0:T(8,128)(2,1)S(1)}, u32[]{:S(2)}, u32[]{:S(2)}) async-start(bf16[8,16,128]{2,1,0:T(8,128)(2,1)} %broadcast_in_dim.153), calls=%async_computation | async-start | bytes 65536 | tf_op jit(solution)/shard_map/all_to_all | solution.py:19
  561.2 6.5 copy.172
  575.0 13.9 %all-to-all-start.14 = ((bf16[8,128,128]{2,1,0:T(8,128)(2,1)}), bf16[8,128,128]{2,1,0:T(8,128)(2,1)S(1)}, u32[]{:S(2)}, u32[]{:S(2)}) async-start(bf16[8,128,128]{2,1,0:T(8,128)(2,1)} %broadcast_in_dim.179), calls=%async_computation.14 | async-start | bytes 524288 | tf_op jit(solution)/shard_map/all_to_all | solution.py:19
  589.4 14.3 %all-to-all-done.14 = bf16[8,128,128]{2,1,0:T(8,128)(2,1)S(1)} async-done(((bf16[8,128,128]{2,1,0:T(8,128)(2,1)}), bf16[8,128,128]{2,1,0:T(8,128)(2,1)S(1)}, u32[]{:S(2)}, u32[]{:S(2)}) %all-to-all-start.14) | async-done | bytes 262176 | tf_op jit(solution)/shard_map/all_to_all | solution.py:19
  603.8 6.4 all_to_all.119
  620.6 14.2 %all-to-all-done.16 = f32[16,1,128]{2,1,0:T(1,128)S(1)} async-done(((f32[16,1,128]{2,1,0:T(1,128)}), f32[16,1,128]{2,1,0:T(1,128)S(1)}, u32[]{:S(2)}, u32[]{:S(2)}) %all-to-all-start.16) | async-done | bytes 8224 | tf_op jit(solution)/shard_map/all_to_all | solution.py:19
  640.3 13.3 %all-to-all-done.17 = f32[16,1,128]{2,1,0:T(1,128)S(1)} async-done(((f32[16,1,128]{2,1,0:T(1,128)}), f32[16,1,128]{2,1,0:T(1,128)S(1)}, u32[]{:S(2)}, u32[]{:S(2)}) %all-to-all-start.17) | async-done | bytes 8224 | tf_op jit(solution)/shard_map/all_to_all | solution.py:19
  658.2 14.0 %all-to-all-done.2 = f32[16,1,16]{2,1,0:T(1,128)S(1)} async-done(((f32[16,1,16]{2,1,0:T(1,128)}), f32[16,1,16]{2,1,0:T(1,128)S(1)}, u32[]{:S(2)}, u32[]{:S(2)}) %all-to-all-start.2) | async-done | bytes 1056 | tf_op jit(solution)/shard_map/all_to_all | solution.py:19
  678.1 12.8 %all-to-all-done.3 = f32[16,1,16]{2,1,0:T(1,128)S(1)} async-done(((f32[16,1,16]{2,1,0:T(1,128)}), f32[16,1,16]{2,1,0:T(1,128)S(1)}, u32[]{:S(2)}, u32[]{:S(2)}) %all-to-all-start.3) | async-done | bytes 1056 | tf_op jit(solution)/shard_map/all_to_all | solution.py:19
  690.9 28.0 %all-to-all-start.18 = ((f32[32,1,1]{2,1,0:T(1,128)}), f32[32,1,1]{2,1,0:T(1,128)S(1)}, u32[]{:S(2)}, u32[]{:S(2)}) async-start(f32[32,1,1]{2,1,0:T(1,128)} %copy.183), calls=%async_computation.18 | async-start | bytes 32768 | tf_op jit(solution)/shard_map/all_to_all | solution.py:201
  719.0 11.4 %all-to-all-done.18 = f32[32,1,1]{2,1,0:T(1,128)S(1)} async-done(((f32[32,1,1]{2,1,0:T(1,128)}), f32[32,1,1]{2,1,0:T(1,128)S(1)}, u32[]{:S(2)}, u32[]{:S(2)}) %all-to-all-start.18) | async-done | bytes 160 | tf_op jit(solution)/shard_map/all_to_all | solution.py:201
  (206 shorter events, 156.4 us)
Async XLA Ops:
  7.2 632.2 %copy-start = (bf16[2048,256]{1,0:T(8,128)(2,1)S(1)}, bf16[2048,256]{1,0:T(8,128)(2,1)}, u32[]{:S(2)}) copy-start(bf16[2048,256]{1,0:T(8,128)(2,1)} %param.20) | copy-start | bytes 3145732
  7.2 288.3 %all-gather.3.cloned.1.call-start = ((), (), s32[]{:S(2)}) async-start(), calls=%async_computation.19 | async-start | bytes 8650752 | tf_op jit(solution)/shard_map/all_gather | solution.py:42
  106.2 52.1 %all-to-all-start.5 = ((bf16[8,512,256]{2,1,0:T(8,128)(2,1)}), bf16[8,512,256]{2,1,0:T(8,128)(2,1)S(1)}, u32[]{:S(2)}, u32[]{:S(2)}) async-start(bf16[8,512,256]{2,1,0:T(8,128)(2,1)} %broadcast_in_dim.166), calls=%async_computation.5 | async-start | bytes 4194304 | tf_op jit(solution)/shard_map/all_to_all | solution.py:19
  111.8 201.8 %copy-start.14 = (pred[16,32]{1,0:T(8,128)(4,1)}, pred[16,32]{1,0:T(8,128)(4,1)S(1)}, u32[]{:S(2)}) copy-start(pred[16,32]{1,0:T(8,128)(4,1)S(1)} %iota_compare_fusion) | copy-start | bytes 1540
  315.9 43.9 %all-to-all-start.7 = ((bf16[8,512,128]{2,1,0:T(8,128)(2,1)}), bf16[8,512,128]{2,1,0:T(8,128)(2,1)S(1)}, u32[]{:S(2)}, u32[]{:S(2)}) async-start(bf16[8,512,128]{2,1,0:T(8,128)(2,1)} %broadcast_in_dim.170), calls=%async_computation.7 | async-start | bytes 2097152 | tf_op jit(solution)/shard_map/all_to_all | solution.py:19
  340.8 59.6 %copy-start.8 = (bf16[16,8,256]{2,1,0:T(8,128)(2,1)}, bf16[16,8,256]{2,1,0:T(8,128)(2,1)S(1)}, u32[]{:S(2)}) copy-start(bf16[16,8,256]{2,1,0:T(8,128)(2,1)S(1)} %gather_fusion.3) | copy-start | bytes 196612
  401.3 29.5 %all-to-all-start.12 = ((bf16[8,128,256]{2,1,0:T(8,128)(2,1)}), bf16[8,128,256]{2,1,0:T(8,128)(2,1)}, u32[]{:S(2)}, u32[]{:S(2)}) async-start(bf16[8,128,256]{2,1,0:T(8,128)(2,1)} %broadcast_in_dim.176), calls=%async_computation.12 | async-start | bytes 1048576 | tf_op jit(solution)/shard_map/all_to_all | solution.py:19
  425.9 58.5 %copy-start.10 = (f32[512,256]{0,1:T(8,128)S(1)}, f32[512,256]{0,1:T(8,128)}, u32[]{:S(2)}) copy-start(f32[512,256]{0,1:T(8,128)} %get-tuple-element.24) | copy-start | bytes 1572868
  480.3 5.8 all-to-all-start.13
  484.6 14.9 %copy-start.5 = (bf16[16,4096]{1,0:T(8,128)(2,1)S(1)}, bf16[16,4096]{1,0:T(8,128)(2,1)}, u32[]{:S(2)}) copy-start(bf16[16,4096]{1,0:T(8,128)(2,1)} %param.17) | copy-start | bytes 393220
  487.8 47.2 %all-to-all-start.10 = ((bf16[8,512,256]{2,1,0:T(8,128)(2,1)}), bf16[8,512,256]{2,1,0:T(8,128)(2,1)S(1)}, u32[]{:S(2)}, u32[]{:S(2)}) async-start(bf16[8,512,256]{2,1,0:T(8,128)(2,1)} %broadcast_in_dim.173), calls=%async_computation.10 | async-start | bytes 4194304 | tf_op jit(solution)/shard_map/all_to_all | solution.py:19
  545.4 28.9 %all-to-all-start = ((bf16[8,16,128]{2,1,0:T(8,128)(2,1)}), bf16[8,16,128]{2,1,0:T(8,128)(2,1)S(1)}, u32[]{:S(2)}, u32[]{:S(2)}) async-start(bf16[8,16,128]{2,1,0:T(8,128)(2,1)} %broadcast_in_dim.153), calls=%async_computation | async-start | bytes 65536 | tf_op jit(solution)/shard_map/all_to_all | solution.py:19
  571.4 17.4 %copy-start.20 = (bf16[256]{0:T(256)(128)(2,1)S(1)}, bf16[256]{0:T(256)(128)(2,1)}, u32[]{:S(2)}) copy-start(bf16[256]{0:T(256)(128)(2,1)} %param.32) | copy-start | bytes 1540
  572.8 16.1 %copy-start.4 = (bf16[32,16384]{1,0:T(8,128)(2,1)S(1)}, bf16[32,16384]{1,0:T(8,128)(2,1)}, u32[]{:S(2)}) copy-start(bf16[32,16384]{1,0:T(8,128)(2,1)} %get-tuple-element.9) | copy-start | bytes 3145732
  575.0 28.7 %all-to-all-start.14 = ((bf16[8,128,128]{2,1,0:T(8,128)(2,1)}), bf16[8,128,128]{2,1,0:T(8,128)(2,1)S(1)}, u32[]{:S(2)}, u32[]{:S(2)}) async-start(bf16[8,128,128]{2,1,0:T(8,128)(2,1)} %broadcast_in_dim.179), calls=%async_computation.14 | async-start | bytes 524288 | tf_op jit(solution)/shard_map/all_to_all | solution.py:19
  589.4 31.2 %copy-start.21 = (bf16[256]{0:T(256)(128)(2,1)S(1)}, bf16[256]{0:T(256)(128)(2,1)}, u32[]{:S(2)}) copy-start(bf16[256]{0:T(256)(128)(2,1)} %param.31) | copy-start | bytes 1540
  603.8 115.1 %copy-start.18 = (s32[16]{0:T(128)S(1)}, s32[16]{0:T(128)}, u32[]{:S(2)}) copy-start(s32[16]{0:T(128)} %copy-done.17) | copy-start | bytes 196
  611.6 4.7 all-to-all-start.1
  617.0 17.8 %all-to-all-start.16 = ((f32[16,1,128]{2,1,0:T(1,128)}), f32[16,1,128]{2,1,0:T(1,128)S(1)}, u32[]{:S(2)}, u32[]{:S(2)}) async-start(f32[16,1,128]{2,1,0:T(1,128)} %broadcast_in_dim.181), calls=%async_computation.16 | async-start | bytes 16384 | tf_op jit(solution)/shard_map/all_to_all | solution.py:19
  635.4 18.2 %all-to-all-start.17 = ((f32[16,1,128]{2,1,0:T(1,128)}), f32[16,1,128]{2,1,0:T(1,128)S(1)}, u32[]{:S(2)}, u32[]{:S(2)}) async-start(f32[16,1,128]{2,1,0:T(1,128)} %broadcast_in_dim.182), calls=%async_computation.17 | async-start | bytes 16384 | tf_op jit(solution)/shard_map/all_to_all | solution.py:19
  654.2 18.1 %all-to-all-start.2 = ((f32[16,1,16]{2,1,0:T(1,128)}), f32[16,1,16]{2,1,0:T(1,128)S(1)}, u32[]{:S(2)}, u32[]{:S(2)}) async-start(f32[16,1,16]{2,1,0:T(1,128)} %broadcast_in_dim.155), calls=%async_computation.2 | async-start | bytes 16384 | tf_op jit(solution)/shard_map/all_to_all | solution.py:19
  672.9 18.0 %all-to-all-start.3 = ((f32[16,1,16]{2,1,0:T(1,128)}), f32[16,1,16]{2,1,0:T(1,128)S(1)}, u32[]{:S(2)}, u32[]{:S(2)}) async-start(f32[16,1,16]{2,1,0:T(1,128)} %broadcast_in_dim.156), calls=%async_computation.3 | async-start | bytes 16384 | tf_op jit(solution)/shard_map/all_to_all | solution.py:19
  676.6 55.3 %copy-start.22 = (f32[16]{0:T(128)}, f32[16]{0:T(128)S(1)}, u32[]{:S(2)}) copy-start(f32[16]{0:T(128)S(1)} %broadcast_multiply_fusion) | copy-start | bytes 196
  690.9 39.5 %all-to-all-start.18 = ((f32[32,1,1]{2,1,0:T(1,128)}), f32[32,1,1]{2,1,0:T(1,128)S(1)}, u32[]{:S(2)}, u32[]{:S(2)}) async-start(f32[32,1,1]{2,1,0:T(1,128)} %copy.183), calls=%async_computation.18 | async-start | bytes 32768 | tf_op jit(solution)/shard_map/all_to_all | solution.py:201
  (13 other events, 44.8 us)
Sparse Core Ops, SparseCore 0:
  12.2 283.1 all-gather.2
where the time goes:
time: 742 us; the launch traced here: 739 us
  waiting for transfers between devices  267 us (36%)
  blocking collectives  189 us (25%)
  starting transfers between devices  125 us (17%)
  local copies, waits for them, and re-layouts  109 us (15%)
  matrix products  22.7 us (3%)
  between operations  14.7 us (2%)
  other arithmetic  10.5 us (1%)
    all_to_all x12, waiting for transfers between devices, sent_to_all(): return lax.all_to_all(copies, axis, split_axis=0, concat_axis=0, tiled=True)  143 us
    all_to_all x5, blocking collectives, sent_to_all(): return lax.all_to_all(copies, axis, split_axis=0, concat_axis=0, tiled=True)  119 us
    all_gather x1, waiting for transfers between devices, gather_packed(): lines, at, done = (lax.all_gather(line, axis), 0, [])  113 us
    all_to_all x12, starting transfers between devices, sent_to_all(): return lax.all_to_all(copies, axis, split_axis=0, concat_axis=0, tiled=True)  97.3 us
    all_to_all x1, blocking collectives, side_by_side(): lax.all_to_all(both, axis, split_axis=split_dim, concat_axis=concat_dim,...  70.6 us
    all_to_all x1, starting transfers between devices, shards(): lax.all_to_all(send_back, 'dp', split_axis=0, concat_axis=0, tiled=True)  28 us
    transpose x5, local copies, waits for them, and re-layouts, joined_along(): return jnp.moveaxis(tiles, 0, dim).reshape(shape)  18.4 us
    unnamed x60, local copies, waits for them, and re-layouts  15.6 us
  transfers between devices with their start and end apart: 14, of which 13 were waited for; matrix products, arithmetic and copies ran while one was open for 14% of the time, Pallas kernels for 0%

commit v1 on v0

v1 whole, which is shorter than its diff:
```python
import functools
import math

import jax
import jax.numpy as jnp
from jax import lax
from jax.experimental import pallas as pl
from jax.experimental.pallas import tpu as pltpu
from jax.sharding import Mesh
from jax.sharding import PartitionSpec as P

D = 4096
HD = 64
EPSILON = 1e-06
AX = ("zl", "x", "y", "zh", "c")
ZL, X, Y, ZH, C = 8, 4, 4, 2, 2
MP = ("y", "zh", "c")
DP = ("zl", "x")
VMEM = pltpu.VMEM
MESH = pl.DeviceIdType.MESH
FLOWS_MP = 22
FLOWS_DP = 74


def hint(value, step):
    return pl.multiple_of(value, step)


class Links:
    def __init__(self, send, recv):
        self.send, self.recv, self.count, self.open = send, recv, 0, []

    def slot(self):
        self.count += 1
        return self.count - 1

    def copy(self, slot, src, dst, to):
        return pltpu.make_async_remote_copy(
            src_ref=src,
            dst_ref=dst,
            send_sem=self.send.at[slot],
            recv_sem=self.recv.at[slot],
            device_id=to,
            device_id_type=MESH,
        )

    def go(self, src, dst, to):
        flow = self.copy(self.slot(), src, dst, to)
        flow.start()
        self.open.append(flow)
        return flow


def gather_kernel(mp, dp, *refs):
    n_mp, n_dp = len(mp), len(dp)
    mp_in, dp_in = refs[:n_mp], refs[n_mp : n_mp + n_dp]
    mp_out = refs[n_mp + n_dp : 2 * n_mp + n_dp]
    dp_out = refs[2 * n_mp + n_dp : 2 * n_mp + 2 * n_dp]
    send, recv, local = refs[2 * (n_mp + n_dp) :]
    zl, x, y, zh, c = (lax.axis_index(a) for a in AX)
    links = Links(send, recv)
    yr, yl, y2 = lax.rem(y + 1, Y), lax.rem(y + Y - 1, Y), lax.rem(y + 2, Y)
    xr, xl = lax.rem(x + 1, X), lax.rem(x + X - 1, X)
    other = 1 - zh
    partner = 1 - c

    barrier = pltpu.get_barrier_semaphore()

    def greet(to):
        pl.semaphore_signal(barrier, inc=1, device_id=to, device_id_type=MESH)

    if n_mp:
        for to in ({"zh": other}, {"y": yr}, {"y": yl}, {"c": partner}):
            greet(to)
    if n_dp:
        greet({"x": xr})
        greet({"x": xl})

        place = zh * ZL + zl
        for step in (1, ZL * ZH - 1):
            near = lax.rem(place + step, ZL * ZH)
            greet({"zh": near // ZL, "zl": lax.rem(near, ZL)})

    homes = []
    for k in range(n_mp):
        width = mp_in[k].shape[1]
        at = hint(((y * ZH + zh) * C + c) * width, 128)
        homes.append(
            pltpu.make_async_copy(mp_in[k], mp_out[k].at[:, pl.ds(at, width)], local.at[k])
        )
    for k in range(n_dp):
        rows = dp_in[k].shape[1]
        at = hint((zl * X + x) * rows, 16)
        homes.append(
            pltpu.make_async_copy(
                dp_in[k], dp_out[k].at[:, pl.ds(at, rows)], local.at[n_mp + k]
            )
        )
    for home in homes:
        home.start()
    pl.semaphore_wait(barrier, 4 * (n_mp > 0) + 4 * (n_dp > 0))

    tasks = []
    arrivals = []
    guarded = []

    def at_time(when, task):
        tasks.append((when, len(tasks), task))

    def mp_chunk(k, r0, n, scale, z_time):
        width = mp_in[k].shape[1]
        half = n // 2

        def full(start, size, yy, hh):
            at = hint(((yy * ZH + hh) * C + c) * width, 128)
            return mp_out[k].at[pl.ds(start, size), pl.ds(at, width)]

        kept = {}

        def to_core(start, size, yy, hh):
            block = full(start, size, yy, hh)
            arrivals.append(links.go(block, block, {"c": partner}))

        def first():
            src = mp_in[k].at[pl.ds(r0, n)]
            dst = full(r0, n, y, zh)
            kept["z"] = links.go(src, dst, {"zh": other})
            kept["r", 0] = links.go(src, dst, {"y": yr})
            kept["l", 0] = links.go(src, dst, {"y": yl})
            arrivals.append(links.go(src, dst, {"c": partner}))

        def second(phase):
            hh = (zh, other)[phase]
            kept["r", phase].wait_recv()
            block = full(r0, half, yl, hh)
            kept["or", phase] = links.go(block, block, {"y": yr})
            to_core(r0, n, yl, hh)
            kept["l", phase].wait_recv()
            block = full(r0 + half, half, yr, hh)
            kept["ol", phase] = links.go(block, block, {"y": yl})
            to_core(r0, n, yr, hh)

        def third(phase):
            hh = (zh, other)[phase]
            kept["or", phase].wait_recv()
            to_core(r0, half, y2, hh)
            kept["ol", phase].wait_recv()
            to_core(r0 + half, half, y2, hh)

        def crossed():
            kept["z"].wait_recv()
            block = full(r0, n, y, other)
            kept["r", 1] = links.go(block, block, {"y": yr})
            kept["l", 1] = links.go(block, block, {"y": yl})
            to_core(r0, n, y, other)

        at_time(-1.0 + r0 * 1e-4, first)
        at_time(scale * (r0 / n + 1), lambda: second(0))
        at_time(scale * (r0 / n + 2), lambda: third(0))
        at_time(z_time, crossed)
        at_time(z_time + scale + 1, lambda: second(1))
        at_time(z_time + 2 * scale + 2, lambda: third(1))

    def dp_array(k, z_step, x_step):
        rows = dp_in[k].shape[1]
        half = rows // 2

        def full(b, xx, start, size):
            at = hint((b * X + xx) * rows + start, 16)
            return dp_out[k].at[:, pl.ds(at, size)]

        z_slots = {(way, s): links.slot() for way in (1, -1) for s in range(ZL - 1)}

        def held(way, s):
            return zl - way * s

        def has(way, s):
            return zl - s >= 0 if way > 0 else zl + s <= ZL - 1

        def room(way):
            return zl < ZL - 1 if way > 0 else zl > 0

        def z_flow(way, s):
            b = held(way, s)
            block = full(b, x, 0, rows)
            src = dp_in[k] if s == 0 else block
            return links.copy(z_slots[way, s], src, block, {"zl": zl + way})

        def z_send(way, s):
            cond = jnp.logical_and(has(way, s), room(way))
            pl.when(cond)(lambda: z_flow(way, s).start())
            guarded.append((cond, lambda: z_flow(way, s).wait_send()))

        def x_block(cond, b, src, when):
            slots = [links.slot() for _ in range(4)]

            def near(way):
                block = full(b, x, 0, rows)
                return links.copy(
                    slots[0 if way > 0 else 1],
                    block if src is None else src,
                    block,
                    {"x": xr if way > 0 else xl},
                )

            def far(way):
                block = full(b, xl if way > 0 else xr, 0 if way > 0 else half, half)
                return links.copy(
                    slots[2 if way > 0 else 3], block, block, {"x": xr if way > 0 else xl}
                )

            def start():
                near(1).start()
                near(-1).start()

            def forward():
                near(1).wait_recv()
                far(1).start()
                near(-1).wait_recv()
                far(-1).start()

            def finish():
                for way in (1, -1):
                    far(way).wait_recv()
                    near(way).wait_send()
                    far(way).wait_send()

            run = (lambda f: f()) if cond is None else (lambda f: pl.when(cond)(f))
            at_time(when + x_step, lambda: run(forward))
            at_time(1e6, lambda: run(finish))
            return start

        def begin():
            for way in (1, -1):
                z_send(way, 0)

        own_start = x_block(None, zl, dp_in[k], 0.0)
        at_time(-2.0 + 0.01 * k, lambda: (begin(), own_start()))

        def z_step_task(way, s):
            cond = has(way, s)
            when = z_step * s
            start = x_block(cond, held(way, s), None, when)

            def task():
                @pl.when(cond)
                def _():
                    block = full(held(way, s), x, 0, rows)
                    links.copy(
                        z_slots[way, s - 1], block, block, {"zl": zl - way}
                    ).wait_recv()

                if s < ZL - 1:
                    z_send(way, s)
                pl.when(cond)(start)

            at_time(when, task)

        for s in range(1, ZL):
            for way in (1, -1):
                z_step_task(way, s)

    for k, spec in enumerate(mp):
        r0 = 0
        for number, n in enumerate(spec["chunks"]):
            mp_chunk(k, r0, n, spec["y_time"], spec["z_time"] * (number + 1))
            r0 += n
    for k, spec in enumerate(dp):
        dp_array(k, spec["z_time"], spec["x_time"])
    for _, _, task in sorted(tasks, key=lambda t: t[:2]):
        task()
    for flow in arrivals:
        flow.wait_recv()
    for flow in links.open:
        flow.wait_send()
    for cond, finish in guarded:
        pl.when(cond)(finish)
    for home in homes:
        home.wait()


def gather(mp_arrays, mp_specs, dp_arrays, dp_specs, collective_id):
    outs = [jax.ShapeDtypeStruct((a.shape[0], a.shape[1] * 16), a.dtype) for a in mp_arrays]
    outs += [
        jax.ShapeDtypeStruct((a.shape[0], a.shape[1] * 32, a.shape[2]), a.dtype)
        for a in dp_arrays
    ]
    slots = FLOWS_MP * sum(len(s["chunks"]) for s in mp_specs) + FLOWS_DP * len(dp_specs)
    count = len(mp_arrays) + len(dp_arrays)
    return pl.pallas_call(
        functools.partial(gather_kernel, mp_specs, dp_specs),
        out_shape=outs,
        in_specs=[pl.BlockSpec(memory_space=VMEM)] * count,
        out_specs=[pl.BlockSpec(memory_space=VMEM)] * count,
        scratch_shapes=[
            pltpu.SemaphoreType.DMA((slots,)),
            pltpu.SemaphoreType.DMA((slots,)),
            pltpu.SemaphoreType.DMA((count,)),
        ],
        compiler_params=pltpu.CompilerParams(
            collective_id=collective_id, has_side_effects=True, vmem_limit_bytes=48 << 20
        ),
        name=f"gather_{collective_id}",
    )(*mp_arrays, *dp_arrays)


def dot(a, b):
    return jnp.dot(a, b, preferred_element_type=jnp.float32)


def dot_t(a, b):
    return lax.dot_general(a, b, (((1,), (1,)), ((), ())), preferred_element_type=jnp.float32)


def of_head(array, head):
    lane = lax.broadcasted_iota(jnp.int32, array.shape, 1)
    return jnp.where((lane >= HD) == (head == 1), array, jnp.zeros_like(array))


def join_heads(first, second):
    lane = lax.broadcasted_iota(jnp.int32, first.shape, 1)
    return jnp.where(lane >= HD, second, first)


def softmax(scores):
    top = jnp.max(scores, axis=1, keepdims=True)
    raised = jnp.exp(scores - top)
    return raised / jnp.sum(raised, axis=1, keepdims=True)


def length_row(lengths, first, count, width):
    col = lax.broadcasted_iota(jnp.int32, (1, width), 1)
    row = jnp.zeros((1, width), jnp.int32)
    for u in range(count):
        row = jnp.where(col // 32 == u, lengths[first + u], row)
    return row


def encoder_kernel(parent, lengths, q, k, v, out):
    group = 4
    for first in range(0, 16, group):
        starts = [hint(parent[first + u] * 32, 32) for u in range(group)]
        queries, keys, values = (
            jnp.concatenate([a[pl.ds(s, 32), :] for s in starts], axis=0) for a in (q, k, v)
        )
        shape = (32 * group, 32 * group)
        row = lax.broadcasted_iota(jnp.int32, shape, 0)
        col = lax.broadcasted_iota(jnp.int32, shape, 1)
        live = (row // 32 == col // 32) & (
            col % 32 < length_row(lengths, first, group, 32 * group)
        )
        heads = []
        for head in range(2):
            scores = dot_t(of_head(queries, head), keys) * (1.0 / math.sqrt(HD))
            weights = softmax(jnp.where(live, scores, -1e30)).astype(jnp.bfloat16)
            heads.append(dot(weights, values))
        out[pl.ds(32 * first, 32 * group), :] = join_heads(*heads).astype(jnp.bfloat16)


def direct_kernel(parent, lengths, q, k, v, cache, out, keys, values):
    for i in range(16):
        keys[pl.ds(32 * i, 32), :] = cache[0, parent[i]]
        values[pl.ds(32 * i, 32), :] = cache[1, parent[i]]
    queries, key_new, value_new = q[...], k[...], v[...].astype(jnp.float32)
    row = lax.broadcasted_iota(jnp.int32, (16, 512), 0)
    col = lax.broadcasted_iota(jnp.int32, (16, 512), 1)
    live = (row == col // 32) & (col % 32 < length_row(lengths, 0, 16, 512))
    heads = []
    for head in range(2):
        mine = of_head(queries, head)
        scores = dot_t(mine, keys[...]) * (1.0 / math.sqrt(HD))
        scores = jnp.where(live, scores, -1e30)
        last = jnp.sum(
            mine.astype(jnp.float32) * key_new.astype(jnp.float32), axis=1, keepdims=True
        ) * (1.0 / math.sqrt(HD))
        top = jnp.maximum(jnp.max(scores, axis=1, keepdims=True), last)
        raised, raised_last = jnp.exp(scores - top), jnp.exp(last - top)
        total = jnp.sum(raised, axis=1, keepdims=True) + raised_last
        weights = (raised / total).astype(jnp.bfloat16)
        weight_last = (raised_last / total).astype(jnp.bfloat16).astype(jnp.float32)
        heads.append(dot(weights, values[...]) + weight_last * value_new)
    out[...] = join_heads(*heads).astype(jnp.bfloat16)


def cross_kernel(lengths, q, k, v, out):
    row = lax.broadcasted_iota(jnp.int32, (128, 512), 0)
    col = lax.broadcasted_iota(jnp.int32, (128, 512), 1)
    live = (row % 16 == col // 32) & (col % 32 < length_row(lengths, 0, 16, 512))
    heads = []
    for head in range(2):
        scores = dot_t(of_head(q[...], head), k[...]) * (1.0 / math.sqrt(HD))
        weights = softmax(jnp.where(live, scores, -1e30)).astype(jnp.bfloat16)
        heads.append(dot(weights, v[...]))
    out[...] = join_heads(*heads).astype(jnp.bfloat16)


def local_call(kernel, out_shape, scalars, arrays, scratch=()):
    return pl.pallas_call(
        kernel,
        out_shape=jax.ShapeDtypeStruct(out_shape, jnp.bfloat16),
        in_specs=[pl.BlockSpec(memory_space=pltpu.SMEM)] * len(scalars)
        + [pl.BlockSpec(memory_space=VMEM)] * len(arrays),
        out_specs=pl.BlockSpec(memory_space=VMEM),
        scratch_shapes=list(scratch),
    )(*scalars, *arrays)


def score_kernel(parts, target, rerank, channel, got, rows, inbox, sends, recvs):
    zl, x, y, zh, c = (lax.axis_index(a) for a in AX)
    me_m = (y * ZH + zh) * C + c
    me_d = zl * X + x
    n_m, n_d = Y * ZH * C, ZL * X

    def to_m(k):
        m = lax.rem(me_m + k, n_m)
        return {"y": m // (ZH * C), "zh": lax.rem(m // C, ZH), "c": lax.rem(m, C)}

    def to_d(k):
        d = lax.rem(me_d + k, n_d)
        return {"zl": d // X, "x": lax.rem(d, X)}

    barrier = pltpu.get_barrier_semaphore()
    for k in range(1, n_m):
        pl.semaphore_signal(barrier, inc=1, device_id=to_m(k), device_id_type=MESH)
    for k in range(1, n_d):
        pl.semaphore_signal(barrier, inc=1, device_id=to_d(k), device_id_type=MESH)
    pl.semaphore_wait(barrier, n_m + n_d - 2)
    flows = []
    for k in range(1, n_m):
        flow = pltpu.make_async_remote_copy(
            src_ref=parts,
            dst_ref=got.at[me_m],
            send_sem=sends.at[k],
            recv_sem=recvs.at[k],
            device_id=to_m(k),
            device_id_type=MESH,
        )
        flow.start()
        flows.append(flow)
    for flow in flows:
        flow.wait_recv()
    total = parts[...]
    for m in range(n_m):
        total = total + jnp.where(me_m == m, 0.0, got[m])
    dots, squares = total[0:8], total[8:16]
    score = jnp.sum(dots / jnp.sqrt(squares / D + EPSILON), axis=0, keepdims=True) / 8
    tail = total[16:24]
    direct = tail[0:1] / jnp.sqrt(tail[1:2] / D + EPSILON)
    rerank[...] = direct + score
    shard = lax.broadcasted_iota(jnp.int32, (n_d, 128), 0)
    slots = jnp.where(shard == target[...], score, 0.0)
    rows[...] = slots
    for k in range(1, n_d):
        d = lax.rem(me_d + k, n_d)
        flow = pltpu.make_async_remote_copy(
            src_ref=rows.at[pl.ds(d, 1)],
            dst_ref=inbox.at[pl.ds(me_d, 1)],
            send_sem=sends.at[n_m + k],
            recv_sem=recvs.at[n_m + k],
            device_id=to_d(k),
            device_id_type=MESH,
        )
        flow.start()
        flows.append(flow)
    for flow in flows[n_m - 1 :]:
        flow.wait_recv()
    mine = shard == me_d
    channel[...] = jnp.sum(jnp.where(mine, slots, inbox[...]), axis=0, keepdims=True)
    for flow in flows:
        flow.wait_send()


def scores(parts, target):
    return pl.pallas_call(
        score_kernel,
        out_shape=[jax.ShapeDtypeStruct((1, 128), jnp.float32)] * 2,
        in_specs=[pl.BlockSpec(memory_space=VMEM)] * 2,
        out_specs=[pl.BlockSpec(memory_space=VMEM)] * 2,
        scratch_shapes=[
            pltpu.VMEM((16, 24, 128), jnp.float32),
            pltpu.VMEM((32, 128), jnp.float32),
            pltpu.VMEM((32, 128), jnp.float32),
            pltpu.SemaphoreType.DMA((48,)),
            pltpu.SemaphoreType.DMA((48,)),
        ],
        compiler_params=pltpu.CompilerParams(collective_id=9, has_side_effects=True),
        name="scores",
    )(parts, target)


def shards(
    hidden,
    wq_direct,
    wkv_direct,
    wo_direct,
    kv_cache,
    parent,
    lengths,
    cand_embed,
    source,
    enc_qkv,
    enc_out,
    cross_q,
    cross_kv,
    cross_out,
    w_direct,
    w_channel,
    target_shard,
):
    bf16 = jnp.bfloat16
    beam_n, len_n, width = cand_embed.shape
    rows_n = beam_n * len_n
    own_start = lax.axis_index(MP) * width
    rows = jnp.concatenate(
        [cand_embed.reshape(rows_n, width), jnp.tile(source[0], (4, 1))], axis=0
    )
    rows_full, qkv_full = gather(
        [rows],
        [dict(chunks=(128, 128, 128, 160), y_time=2.0, z_time=9.0)],
        [enc_qkv],
        [dict(z_time=5.0, x_time=4.0)],
        1,
    )
    query_new = dot(hidden, wq_direct).astype(bf16)
    key_new = dot(hidden, wkv_direct[0]).astype(bf16)
    value_new = dot(hidden, wkv_direct[1]).astype(bf16)
    local = pltpu.VMEM((rows_n, 2 * HD), bf16)
    direct_context = local_call(
        direct_kernel,
        (beam_n, 2 * HD),
        [parent, lengths],
        [query_new, key_new, value_new, kv_cache],
        [local, local],
    )
    tokens_full = rows_full[:rows_n]
    enc = [dot(tokens_full, qkv_full[j]).astype(bf16) for j in range(3)]
    enc_context = local_call(encoder_kernel, (rows_n, 2 * HD), [parent, lengths], enc)
    contexts = jnp.concatenate(
        [enc_context, direct_context, jnp.zeros_like(direct_context)], axis=0
    )
    context_full, out_full, query_full = gather(
        [contexts],
        [dict(chunks=(256, 288), y_time=2.0, z_time=7.0)],
        [enc_out[None], cross_q[None]],
        [dict(z_time=2.0, x_time=1.5), dict(z_time=2.1, x_time=1.6)],
        2,
    )
    hidden_share = lax.dynamic_slice_in_dim(hidden, own_start, width, 1).astype(jnp.float32)
    new_state = hidden_share + dot(context_full[rows_n : rows_n + beam_n], wo_direct)
    tokens = cand_embed[parent].reshape(rows_n, width)
    summed = tokens.astype(jnp.float32) + dot(context_full[:rows_n], out_full[0])
    cross_queries = dot(rows_full[rows_n : rows_n + 8], query_full[0]).astype(bf16)
    summed_full, memory_full, cross_full = gather(
        [summed.astype(bf16)],
        [dict(chunks=(128,) * 4, y_time=2.0, z_time=9.0)],
        [cross_kv, cross_out[None]],
        [dict(z_time=5.0, x_time=3.0), dict(z_time=5.1, x_time=3.1)],
        3,
    )
    wide = summed_full.astype(jnp.float32)
    norm = jnp.sqrt(jnp.mean(wide * wide, axis=1, keepdims=True) + EPSILON)
    cross_keys = (dot(summed_full, memory_full[0]) / norm).astype(bf16)
    cross_values = (dot(summed_full, memory_full[1]) / norm).astype(bf16)
    cross_context = local_call(
        cross_kernel,
        (8 * beam_n, 2 * HD),
        [lengths],
        [jnp.repeat(cross_queries, beam_n, axis=0), cross_keys, cross_values],
    )
    (cross_context_full,) = gather(
        [cross_context], [dict(chunks=(128,), y_time=2.0, z_time=5.0)], [], [], 4
    )
    decoded = dot(cross_context_full, cross_full[0]).reshape(8, beam_n, width)
    decoded = decoded + source[0].astype(jnp.float32)[:, None]
    parts = jnp.concatenate(
        [
            jnp.sum(decoded * w_channel.astype(jnp.float32), axis=2),
            jnp.sum(decoded * decoded, axis=2),
            jnp.sum(new_state * w_direct.astype(jnp.float32), axis=1)[None],
            jnp.sum(new_state * new_state, axis=1)[None],
        ],
        axis=0,
    )
    parts = jnp.pad(parts, ((0, 6), (0, 128 - beam_n)))
    target = jnp.pad(target_shard[None], ((0, 0), (0, 128 - beam_n)), constant_values=-1)
    rerank, channel = scores(parts, target)
    return (new_state.astype(bf16), rerank[0, :beam_n], channel[0, :beam_n])


def solution(mesh):
    split = Mesh(mesh.devices.reshape(ZL, X, Y, ZH, C), AX)
    in_specs = (
        P(DP, None),
        P(None, MP),
        P(None, None, MP),
        P(None, MP),
        P(None, DP, None, MP),
        P(DP),
        P(DP),
        P(DP, None, MP),
        P(DP, None, MP),
        P(None, DP, MP),
        P(DP, MP),
        P(DP, MP),
        P(None, DP, MP),
        P(DP, MP),
        P(MP),
        P(MP),
        P(DP),
    )
    out_specs = (P(DP, MP), P(DP), P(DP))
    return jax.shard_map(
        shards, mesh=split, in_specs=in_specs, out_specs=out_specs, check_vma=False
    )
```

time: 742 us -> 322 us (0.43)
  Pallas kernels: 0 us -> 282 us
  waiting for transfers between devices: 267 us -> 0 us
  blocking collectives: 189 us -> 0 us
  starting transfers between devices: 125 us -> 0 us
  local copies, waits for them, and re-layouts: 109 us -> 7.02 us
  between operations: 14.7 us -> 0.85 us
    pallas_call x0 -> x8, Pallas kernels: none -> 282 us  [the longest x4 243 us: gather(): pl.pallas_call(functools.partial(gather_kernel, mp_specs, dp_specs), out_...]
    all_to_all x6 -> x0, blocking collectives: 189 us -> none  [the longest x5 119 us: sent_to_all(): return lax.all_to_all(copies, axis, split_axis=0, concat_axis=0, tiled=True)]
    all_to_all x13 -> x0, waiting for transfers between devices: 154 us -> none  [the longest x12 143 us: sent_to_all(): return lax.all_to_all(copies, axis, split_axis=0, concat_axis=0, tiled=True)]
    all_to_all x13 -> x0, starting transfers between devices: 125 us -> none  [the longest x12 97.3 us: sent_to_all(): return lax.all_to_all(copies, axis, split_axis=0, concat_axis=0, tiled=True)]
    all_gather x1 -> x0, waiting for transfers between devices: 113 us -> none  [gather_packed(): lines, at, done = (lax.all_gather(line, axis), 0, [])]
    transpose x5 -> x0, local copies, waits for them, and re-layouts: 18.4 us -> none  [joined_along(): return jnp.moveaxis(tiles, 0, dim).reshape(shape)]
    all_to_all x9 -> x0, local copies, waits for them, and re-layouts: 15.3 us -> none  [the longest x6 10.6 us: sent_to_all(): return lax.all_to_all(copies, axis, split_axis=0, concat_axis=0, tiled=True)]
    broadcast_in_dim x20 -> x2, local copies, waits for them, and re-layouts: 14.6 us -> 0.62 us  [the longest x1 0.62 us: shards(): jnp.repeat(cross_queries, beam_n, axis=0)]
  transfers between devices with their start and end apart: 14 -> 0, of which waited for: 13 -> 0; matrix products, arithmetic and copies ran while one was open for 14% -> 0% of each run, Pallas kernels for 0% -> 0%
where the time goes in v1:
time: 322 us; the launch traced here: 321 us
  Pallas kernels  282 us (88%)
  matrix products  23.9 us (7%)
  local copies, waits for them, and re-layouts  7.02 us (2%)
  other arithmetic  6.66 us (2%)
    pallas_call x4, Pallas kernels, gather(): pl.pallas_call(functools.partial(gather_kernel, mp_specs, dp_specs), out_...  243 us
    pallas_call x1, Pallas kernels, scores(): pl.pallas_call(score_kernel, out_shape=[jax.ShapeDtypeStruct((1, 128), jn...  30.1 us
    dot_general x12, matrix products, dot(): return jnp.dot(a, b, preferred_element_type=jnp.float32)  23.9 us
    pallas_call x3, Pallas kernels, local_call(): pl.pallas_call(kernel, out_shape=jax.ShapeDtypeStruct(out_shape, jnp.bflo...  9.18 us

profile of v1, /device:TPU:1, one launch (start us, length us, event | category | flops | bytes accessed | tf_op | source)
XLA Modules:
  0.0 320.7 jit_solution(1897822943985046525)
XLA Ops:
  1.4 2.2 convolution_convert_fusion.2.q
  3.6 2.1 convolution_convert_fusion.1.k
  5.7 2.2 convolution_convert_fusion.v
  7.9 2.4 shard_map.185
  11.9 85.4 %gather_1.1 = (bf16[544,4096]{1,0:T(8,128)(2,1)}, bf16[3,4096,128]{2,1,0:T(8,128)(2,1)S(1)}) custom-call(bf16[544,256]{1,0:T(8,128)(2,1)S(1)} %pad_maximum_fusion.refs_0_, bf16[3,128,128]{2,1,0:T(8,128)(2,1)S(1)} %copy-done.2), custom_call_target="tpu_custom_call" | custom-call | tf_op jit(solution)/shard_map/gather_1/pallas_call | solution.py:290
  97.3 4.2 %fusion.14.q = bf16[512,128]{1,0:T(8,128)(2,1)} fusion(bf16[544,4096]{1,0:T(8,128)(2,1)} %get-tuple-element.13, bf16[3,4096,128]{2,1,0:T(8,128)(2,1)S(1)} %get-tuple-element.14), kind=kOutput, calls=%fused_computation.14 | convolution fusion | flops 536936448 | bytes 5373952 | tf_op jit(solution)/shard_map/dot_general | solution.py:308
  101.6 1.9 fusion.17.k
  103.5 1.9 fusion.20.v
  105.4 4.4 %shard_map.184 = bf16[512,128]{1,0:T(8,128)(2,1)} custom-call(s32[16]{0:T(128)} %parent.3, s32[16]{0:T(128)} %lengths.5, bf16[512,128]{1,0:T(8,128)(2,1)} %fusion.14.q, bf16[512,128]{1,0:T(8,128)(2,1)} %fusion.17.k, bf16[512,128]{1,0:T(8,128)(2,1)} %fusion.20.v), custom_call_target="tpu_custom_call" | custom-call | tf_op jit(solution)/shard_map/pallas_call | solution.py:398
  109.9 1.1 maximum_maximum_fusion.refs_0_
  111.0 57.6 %gather_2.1 = (bf16[544,2048]{1,0:T(8,128)(2,1)S(1)}, bf16[1,2048,256]{2,1,0:T(8,128)(2,1)S(1)}, bf16[1,4096,128]{2,1,0:T(8,128)(2,1)S(1)}) custom-call(bf16[544,128]{1,0:T(8,128)(2,1)S(1)} %maximum_maximum_fusion.refs_0_, bf16[1,64,256]{2,1,0:T(8,128)(2,1)S(1)} %bitcast.61, bf16[1,128,128]{2,1,0:T(8,128)(2,1)S(1)} %bitcast.62), custom_call_target="tpu_custom_call" | custom-call | tf_op jit(solution)/shard_map/gather_2/pallas_call | solution.py:290
  168.6 1.4 copy-done.7
  170.0 1.8 multiply_reduce_fusion.4
  171.8 1.1 convolution_convert_fusion.3
  173.5 1.5 gather_fusion
  175.1 2.3 fusion.11.refs_0_
  177.4 80.0 %gather_3.1 = (bf16[512,4096]{1,0:T(8,128)(2,1)}, bf16[2,4096,128]{2,1,0:T(8,128)(2,1)S(1)}, bf16[1,2048,256]{2,1,0:T(8,128)(2,1)S(1)}) custom-call(bf16[512,256]{1,0:T(8,128)(2,1)S(1)} %fusion.11.refs_0_, bf16[2,128,128]{2,1,0:T(8,128)(2,1)S(1)} %copy-done.3, bf16[1,64,256]{2,1,0:T(8,128)(2,1)S(1)} %bitcast.63), custom_call_target="tpu_custom_call" | custom-call | tf_op jit(solution)/shard_map/gather_3/pallas_call | solution.py:290
  257.4 3.2 %multiply_reduce_fusion = f32[512]{0:T(512)S(1)} fusion(bf16[512,4096]{1,0:T(8,128)(2,1)} %get-tuple-element.18), kind=kLoop, calls=%fused_computation.1 | loop fusion | flops 6290944 | bytes 4196352 | tf_op jit(solution)/shard_map/reduce_sum | solution.py:561
  260.8 1.9 fusion.23.k
  262.7 1.9 fusion.24.v
  264.6 2.4 shard_map.186.refs_0_
  267.8 20.1 %gather_4.1 = bf16[128,2048]{1,0:T(8,128)(2,1)S(1)} custom-call(bf16[128,128]{1,0:T(8,128)(2,1)S(1)} %copy-done.1), custom_call_target="tpu_custom_call" | custom-call | tf_op jit(solution)/shard_map/gather_4/pallas_call | solution.py:290
  289.4 30.1 %scores.1 = (f32[1,128]{1,0:T(1,128)}, f32[1,128]{1,0:T(1,128)}) custom-call(f32[24,128]{1,0:T(8,128)} %select_maximum_fusion.parts, s32[1,128]{1,0:T(1,128)} %pad.9.target), custom_call_target="tpu_custom_call" | custom-call | tf_op jit(solution)/shard_map/scores/pallas_call | solution.py:474
  319.6 1.2 slice_bitcast_fusion
  (43 shorter events, 5.7 us)
Async XLA Ops:
  0.6 169.3 %copy-start = (bf16[2048,256]{1,0:T(8,128)(2,1)S(1)}, bf16[2048,256]{1,0:T(8,128)(2,1)}, u32[]{:S(2)}) copy-start(bf16[2048,256]{1,0:T(8,128)(2,1)} %param.20) | copy-start | bytes 3145732
  0.6 11.3 %copy-start.2 = (bf16[3,128,128]{2,1,0:T(8,128)(2,1)S(1)}, bf16[3,128,128]{2,1,0:T(8,128)(2,1)}, u32[]{:S(2)}) copy-start(bf16[3,128,128]{2,1,0:T(8,128)(2,1)} %refs_1_.2) | copy-start | bytes 294916
  97.3 4.3 %copy-start.12 = (bf16[544,4096]{1,0:T(8,128)(2,1)S(1)}, bf16[544,4096]{1,0:T(8,128)(2,1)}, u32[]{:S(2)}) copy-start(bf16[544,4096]{1,0:T(8,128)(2,1)} %get-tuple-element.13) | copy-start | bytes 13369348
  103.5 6.4 %copy-start.9 = (bf16[16,128]{1,0:T(8,128)(2,1)S(1)}, bf16[16,128]{1,0:T(8,128)(2,1)}, u32[]{:S(2)}) copy-start(bf16[16,128]{1,0:T(8,128)(2,1)} %shard_map.185) | copy-start | bytes 12292
  103.5 7.5 %copy-start.4 = (bf16[64,256]{1,0:T(8,128)(2,1)S(1)}, bf16[64,256]{1,0:T(8,128)(2,1)}, u32[]{:S(2)}) copy-start(bf16[64,256]{1,0:T(8,128)(2,1)} %param.27) | copy-start | bytes 98308
  103.5 7.5 %copy-start.5 = (bf16[128,128]{1,0:T(8,128)(2,1)S(1)}, bf16[128,128]{1,0:T(8,128)(2,1)}, u32[]{:S(2)}) copy-start(bf16[128,128]{1,0:T(8,128)(2,1)} %param.28) | copy-start | bytes 98308
  103.5 68.3 %copy-start.13 = (bf16[256]{0:T(256)(128)(2,1)S(1)}, bf16[256]{0:T(256)(128)(2,1)}, u32[]{:S(2)}) copy-start(bf16[256]{0:T(256)(128)(2,1)} %param.32) | copy-start | bytes 1540
  103.5 68.3 %copy-start.10 = (bf16[1,8,256]{2,1,0:T(8,128)(2,1)S(1)}, bf16[1,8,256]{2,1,0:T(8,128)(2,1)}, u32[]{:S(2)}) copy-start(bf16[1,8,256]{2,1,0:T(8,128)(2,1)} %param.25) | copy-start | bytes 12292
  103.5 70.0 %copy-start.11 = (s32[16]{0:T(128)S(1)}, s32[16]{0:T(128)}, u32[]{:S(2)}) copy-start(s32[16]{0:T(128)} %parent.3) | copy-start | bytes 196
  109.9 67.5 %copy-start.3 = (bf16[2,128,128]{2,1,0:T(8,128)(2,1)S(1)}, bf16[2,128,128]{2,1,0:T(8,128)(2,1)}, u32[]{:S(2)}) copy-start(bf16[2,128,128]{2,1,0:T(8,128)(2,1)} %refs_1_.3) | copy-start | bytes 196612
  109.9 67.5 %copy-start.6 = (bf16[64,256]{1,0:T(8,128)(2,1)S(1)}, bf16[64,256]{1,0:T(8,128)(2,1)}, u32[]{:S(2)}) copy-start(bf16[64,256]{1,0:T(8,128)(2,1)} %param.30) | copy-start | bytes 98308
  168.6 1.4 copy-start.7
  257.4 3.5 %copy-start.8 = (bf16[512,4096]{1,0:T(8,128)(2,1)S(1)}, bf16[512,4096]{1,0:T(8,128)(2,1)}, u32[]{:S(2)}) copy-start(bf16[512,4096]{1,0:T(8,128)(2,1)} %get-tuple-element.18) | copy-start | bytes 12582916
  262.7 26.2 %copy-start.14 = (s32[16]{0:T(128)S(1)}, s32[16]{0:T(128)}, u32[]{:S(2)}) copy-start(s32[16]{0:T(128)} %param.33) | copy-start | bytes 196
  267.1 0.8 copy-start.1

commit v2 on v1

v2 whole, which is shorter than its diff:
```python
import functools
import math

import jax
import jax.numpy as jnp
from jax import lax
from jax.experimental import pallas as pl
from jax.experimental.pallas import tpu as pltpu
from jax.sharding import Mesh
from jax.sharding import PartitionSpec as P

D = 4096
HD = 64
EPSILON = 1e-06
AX = ("zl", "x", "y", "zh", "c")
ZL, X, Y, ZH, C = 8, 4, 4, 2, 2
MP = ("y", "zh", "c")
DP = ("zl", "x")
VMEM = pltpu.VMEM
LAG = 4
MESH = pl.DeviceIdType.MESH


def hint(value, step):
    return pl.multiple_of(value, step)


def gather_kernel(chunks, plan, n_dp, *refs):
    mp_in, dp_in = refs[0], refs[1 : 1 + n_dp]
    mp_out, dp_out = refs[1 + n_dp], refs[2 + n_dp : 2 + 2 * n_dp]
    send, recv, local = refs[2 + 2 * n_dp :]
    zl, x, y, zh, c = (lax.axis_index(a) for a in AX)
    yr, yl, y2 = lax.rem(y + 1, Y), lax.rem(y + Y - 1, Y), lax.rem(y + 2, Y)
    xr, xl = lax.rem(x + 1, X), lax.rem(x + X - 1, X)
    other = 1 - zh
    to_y = {1: {"y": yr}, -1: {"y": yl}}
    to_x = {1: {"x": xr}, -1: {"x": xl}}
    to_z = {}
    for way in (1, -1):
        near = lax.rem(zh * ZL + zl + way + ZL * ZH, ZL * ZH)
        to_z[way] = {"zh": near // ZL, "zl": lax.rem(near, ZL)}
    to_other = {"zh": other}
    to_partner = {"c": 1 - c}
    width = mp_in.shape[1]
    n = mp_in.shape[0] // chunks
    first = n // 32 * 16

    def column(yy, hh):
        return pl.ds(hint(((yy * ZH + hh) * C + c) * width, 128), width)

    def block(k, b, xx, start, size):
        rows = dp_in[k].shape[1]
        return dp_out[k].at[:, pl.ds(hint((b * X + xx) * rows + start, 16), size)]

    homes = [pltpu.make_async_copy(mp_in, mp_out.at[:, column(y, zh)], local.at[0])]
    for k in range(n_dp):
        homes.append(
            pltpu.make_async_copy(
                dp_in[k], block(k, zl, x, 0, dp_in[k].shape[1]), local.at[1 + k]
            )
        )
    for home in homes:
        home.start()

    barrier = pltpu.get_barrier_semaphore()
    peers = [to_other, to_y[1], to_y[-1], to_partner]
    if n_dp:
        peers += [to_x[1], to_x[-1]]
        peers += [to_z[1], to_z[-1]]
    for peer in peers:
        pl.semaphore_signal(barrier, inc=1, device_id=peer, device_id_type=MESH)
    pl.semaphore_wait(barrier, len(peers))
    for home in homes:
        home.wait()

    def copy(slot, ref, to):
        return pltpu.make_async_remote_copy(
            src_ref=ref,
            dst_ref=ref,
            send_sem=send.at[slot],
            recv_sem=recv.at[slot],
            device_id=to,
            device_id_type=MESH,
        )

    whole, low, high = (0, n), (0, first), (first, n - first)
    table = {
        "z": (whole, y, 0, to_other),
        "r": (whole, y, 1, to_y[1]),
        "l": (whole, y, 1, to_y[-1]),
        "c": (whole, y, 1, to_partner),
        "cl": (whole, yl, 1, to_partner),
        "cr": (whole, yr, 1, to_partner),
        "co": (whole, y2, 1, to_partner),
        "or": (low, yl, 1, to_y[1]),
        "ol": (high, yr, 1, to_y[-1]),
    }
    order = {name: i for i, name in enumerate(table)}
    n_kinds = 2 * len(table)

    def mp_slot(name, phase, j):
        return (order[name] * 2 + phase) * chunks + j

    def flow(name, phase, j):
        (start, size), yy, _, to = table[name]
        hh = lax.rem(zh + phase, ZH)
        rows = pl.ds(hint(j * n + start, 16), size)
        return copy(mp_slot(name, phase, j), mp_out.at[rows, column(yy, hh)], to)

    def loop(start, stop, body):
        def step(j, carry):
            body(j + start)
            return carry

        lax.fori_loop(0, stop - start, step, 0)

    def each(body):
        loop(0, chunks, body)

    def open_phase(phase, j):
        for name in ("r", "l", "c"):
            flow(name, phase, j).start()

    def cross(j):
        flow("z", 0, j).start()

    def open_other(j):
        flow("z", 0, j).wait_recv()
        open_phase(1, j)

    def pass_on(phase, j):
        flow("r", phase, j).wait_recv()
        flow("or", phase, j).start()
        flow("cl", phase, j).start()
        flow("l", phase, j).wait_recv()
        flow("ol", phase, j).start()
        flow("cr", phase, j).start()

    def take_far(phase, j):
        flow("or", phase, j).wait_recv()
        flow("ol", phase, j).wait_recv()
        flow("co", phase, j).start()

    def close_all():
        each(lambda j: flow("z", 0, j).wait_send())

        def close(phase):
            def body(j):
                for name in table:
                    if name != "z":
                        if name[0] == "c":
                            flow(name, phase, j).wait_recv()
                        flow(name, phase, j).wait_send()

            each(body)

        loop(0, 2, close)

    if not n_dp:
        each(cross)
    each(functools.partial(open_phase, 0))
    if not n_dp:

        def phase_step(phase):
            @pl.when(phase == 1)
            def _():
                each(open_other)

            each(functools.partial(pass_on, phase))
            each(functools.partial(take_far, phase))

        loop(0, 2, phase_step)
        close_all()
        return

    z_base = n_kinds * chunks
    x_base = z_base + 2 * ZL * n_dp
    ways = (1, -1)

    def has(way, s):
        return (zl - s >= 0) if way > 0 else ((zl + s <= ZL - 1) & (s >= 1))

    def sends(way, s):
        return (zl - s >= 0) & (zl < ZL - 1) if way > 0 else (zl + s <= ZL - 1) & (zl > 0)

    def held(way, s):
        return lax.rem(zl - way * s + 2 * ZL, ZL)

    def z_flow(way, s, k, b, to):
        slot = z_base + (ZL if way < 0 else 0) * n_dp + s * n_dp + k
        return copy(slot, block(k, b, x, 0, dp_in[k].shape[1]), to)

    def x_flow(way, s, k, kind):
        rows = dp_in[k].shape[1]
        half = rows // 2
        slot = x_base + (((way < 0) * ZL + s) * n_dp + k) * 4 + kind
        b = held(way, s)
        xx, start, size, side = (
            (x, 0, rows, 1),
            (x, 0, rows, -1),
            (xl, 0, half, 1),
            (xr, half, half, -1),
        )[kind]
        return copy(slot, block(k, b, xx, start, size), to_x[side])

    for way in ways:

        @pl.when(sends(way, 0))
        def _():
            for k in range(n_dp):
                z_flow(way, 0, k, zl, to_z[way]).start()

    for k in range(n_dp):
        x_flow(1, 0, k, 0).start()
        x_flow(1, 0, k, 1).start()

    lag = LAG

    def line_step(step, carry):
        beat = step + 1
        s = lax.rem(beat, ZL)
        for way in ways:

            @pl.when((beat <= ZL - 1) & has(way, s))
            def _():
                for k in range(n_dp):
                    z_flow(way, s - 1, k, held(way, s), to_z[-way]).wait_recv()

                    @pl.when((s < ZL - 1) & sends(way, s))
                    def _():
                        z_flow(way, s, k, held(way, s), to_z[way]).start()

                    x_flow(way, s, k, 0).start()
                    x_flow(way, s, k, 1).start()

        t = lax.rem(beat + 2 * ZL - lag, ZL)
        for way in ways:

            @pl.when((beat >= lag) & has(way, t))
            def _():
                for k in range(n_dp):
                    x_flow(way, t, k, 0).wait_recv()
                    x_flow(way, t, k, 2).start()
                    x_flow(way, t, k, 1).wait_recv()
                    x_flow(way, t, k, 3).start()

        pass_0, far_0, go_z, start_1, pass_1, far_1 = plan
        pl.when(beat == go_z)(lambda: each(cross))
        pl.when(beat == start_1)(lambda: each(open_other))

        @pl.when((beat == pass_0) | (beat == pass_1))
        def _():
            each(functools.partial(pass_on, lax.div(beat, pass_1)))

        @pl.when((beat == far_0) | (beat == far_1))
        def _():
            each(functools.partial(take_far, lax.div(beat, far_1)))

        return carry

    lax.fori_loop(0, ZL + lag - 1, line_step, 0)

    def line_close(s, carry):
        for way in ways:

            @pl.when(has(way, s))
            def _():
                for k in range(n_dp):
                    for kind in range(4):
                        if kind > 1:
                            x_flow(way, s, k, kind).wait_recv()
                        x_flow(way, s, k, kind).wait_send()

            @pl.when((s < ZL - 1) & sends(way, s))
            def _():
                for k in range(n_dp):
                    z_flow(way, s, k, held(way, s), to_z[way]).wait_send()

        return carry

    lax.fori_loop(0, ZL, line_close, 0)
    close_all()


def gather(rows, chunks, plan, weights, collective_id):
    outs = [jax.ShapeDtypeStruct((rows.shape[0], rows.shape[1] * 16), rows.dtype)]
    outs += [
        jax.ShapeDtypeStruct((a.shape[0], a.shape[1] * 32, a.shape[2]), a.dtype) for a in weights
    ]
    n_dp = len(weights)
    slots = 18 * chunks + (2 * ZL + 8 * ZL) * n_dp
    return pl.pallas_call(
        functools.partial(gather_kernel, chunks, plan, n_dp),
        out_shape=outs,
        in_specs=[pl.BlockSpec(memory_space=VMEM)] * (1 + n_dp),
        out_specs=[pl.BlockSpec(memory_space=VMEM)] * (1 + n_dp),
        scratch_shapes=[
            pltpu.SemaphoreType.DMA((slots,)),
            pltpu.SemaphoreType.DMA((slots,)),
            pltpu.SemaphoreType.DMA((1 + n_dp,)),
        ],
        compiler_params=pltpu.CompilerParams(
            collective_id=collective_id, has_side_effects=True, vmem_limit_bytes=48 << 20
        ),
        name=f"gather_{collective_id}",
    )(rows, *weights)


def dot(a, b):
    return jnp.dot(a, b, preferred_element_type=jnp.float32)


def dot_t(a, b):
    return lax.dot_general(a, b, (((1,), (1,)), ((), ())), preferred_element_type=jnp.float32)


def of_head(array, head):
    lane = lax.broadcasted_iota(jnp.int32, array.shape, 1)
    return jnp.where((lane >= HD) == (head == 1), array, jnp.zeros_like(array))


def join_heads(first, second):
    lane = lax.broadcasted_iota(jnp.int32, first.shape, 1)
    return jnp.where(lane >= HD, second, first)


def softmax(scores):
    top = jnp.max(scores, axis=1, keepdims=True)
    raised = jnp.exp(scores - top)
    return raised / jnp.sum(raised, axis=1, keepdims=True)


def length_row(lengths, first, count, width):
    col = lax.broadcasted_iota(jnp.int32, (1, width), 1)
    row = jnp.zeros((1, width), jnp.int32)
    for u in range(count):
        row = jnp.where(col // 32 == u, lengths[first + u], row)
    return row


def encoder_kernel(parent, lengths, enc, out):
    group = 4
    for first in range(0, 16, group):
        starts = [hint(parent[first + u] * 32, 32) for u in range(group)]
        queries, keys, values = (
            jnp.concatenate([enc[pl.ds(s, 32), pl.ds(at, 128)] for s in starts], axis=0)
            for at in (0, 128, 256)
        )
        shape = (32 * group, 32 * group)
        row = lax.broadcasted_iota(jnp.int32, shape, 0)
        col = lax.broadcasted_iota(jnp.int32, shape, 1)
        live = (row // 32 == col // 32) & (
            col % 32 < length_row(lengths, first, group, 32 * group)
        )
        heads = []
        for head in range(2):
            scores = dot_t(of_head(queries, head), keys) * (1.0 / math.sqrt(HD))
            weights = softmax(jnp.where(live, scores, -1e30)).astype(jnp.bfloat16)
            heads.append(dot(weights, values))
        out[pl.ds(32 * first, 32 * group), :] = join_heads(*heads).astype(jnp.bfloat16)


def direct_kernel(parent, lengths, q, k, v, cache, out, keys, values):
    for i in range(16):
        keys[pl.ds(32 * i, 32), :] = cache[0, parent[i]]
        values[pl.ds(32 * i, 32), :] = cache[1, parent[i]]
    queries, key_new, value_new = q[...], k[...], v[...].astype(jnp.float32)
    row = lax.broadcasted_iota(jnp.int32, (16, 512), 0)
    col = lax.broadcasted_iota(jnp.int32, (16, 512), 1)
    live = (row == col // 32) & (col % 32 < length_row(lengths, 0, 16, 512))
    heads = []
    for head in range(2):
        mine = of_head(queries, head)
        scores = dot_t(mine, keys[...]) * (1.0 / math.sqrt(HD))
        scores = jnp.where(live, scores, -1e30)
        last = jnp.sum(
            mine.astype(jnp.float32) * key_new.astype(jnp.float32), axis=1, keepdims=True
        ) * (1.0 / math.sqrt(HD))
        top = jnp.maximum(jnp.max(scores, axis=1, keepdims=True), last)
        raised, raised_last = jnp.exp(scores - top), jnp.exp(last - top)
        total = jnp.sum(raised, axis=1, keepdims=True) + raised_last
        weights = (raised / total).astype(jnp.bfloat16)
        weight_last = (raised_last / total).astype(jnp.bfloat16).astype(jnp.float32)
        heads.append(dot(weights, values[...]) + weight_last * value_new)
    out[...] = join_heads(*heads).astype(jnp.bfloat16)


def cross_kernel(lengths, q, kv, out):
    k, v = kv[:, 0:128], kv[:, 128:256]
    row = lax.broadcasted_iota(jnp.int32, (128, 512), 0)
    col = lax.broadcasted_iota(jnp.int32, (128, 512), 1)
    live = (row % 16 == col // 32) & (col % 32 < length_row(lengths, 0, 16, 512))
    heads = []
    for head in range(2):
        scores = dot_t(of_head(q[...], head), k) * (1.0 / math.sqrt(HD))
        weights = softmax(jnp.where(live, scores, -1e30)).astype(jnp.bfloat16)
        heads.append(dot(weights, v))
    out[...] = join_heads(*heads).astype(jnp.bfloat16)


def local_call(kernel, out_shape, scalars, arrays, scratch=()):
    return pl.pallas_call(
        kernel,
        out_shape=jax.ShapeDtypeStruct(out_shape, jnp.bfloat16),
        in_specs=[pl.BlockSpec(memory_space=pltpu.SMEM)] * len(scalars)
        + [pl.BlockSpec(memory_space=VMEM)] * len(arrays),
        out_specs=pl.BlockSpec(memory_space=VMEM),
        scratch_shapes=list(scratch),
    )(*scalars, *arrays)


def score_kernel(parts, target, rerank, channel, got, rows, inbox, sends, recvs):
    zl, x, y, zh, c = (lax.axis_index(a) for a in AX)
    me_m = (y * ZH + zh) * C + c
    me_d = zl * X + x
    n_m, n_d = Y * ZH * C, ZL * X

    def to_m(k):
        m = lax.rem(me_m + k, n_m)
        return {"y": m // (ZH * C), "zh": lax.rem(m // C, ZH), "c": lax.rem(m, C)}

    def to_d(k):
        d = lax.rem(me_d + k, n_d)
        return {"zl": d // X, "x": lax.rem(d, X)}

    def loop(start, stop, body):
        def step(k, carry):
            body(k + start)
            return carry

        lax.fori_loop(0, stop - start, step, 0)

    barrier = pltpu.get_barrier_semaphore()

    def greet(to):
        pl.semaphore_signal(barrier, inc=1, device_id=to, device_id_type=MESH)

    loop(1, n_m, lambda k: greet(to_m(k)))
    loop(1, n_d, lambda k: greet(to_d(k)))
    pl.semaphore_wait(barrier, n_m + n_d - 2)

    def part_flow(k):
        return pltpu.make_async_remote_copy(
            src_ref=parts,
            dst_ref=got.at[me_m],
            send_sem=sends.at[k],
            recv_sem=recvs.at[k],
            device_id=to_m(k),
            device_id_type=MESH,
        )

    def score_flow(k):
        return pltpu.make_async_remote_copy(
            src_ref=rows.at[pl.ds(lax.rem(me_d + k, n_d), 1)],
            dst_ref=inbox.at[pl.ds(me_d, 1)],
            send_sem=sends.at[n_m + k],
            recv_sem=recvs.at[n_m + k],
            device_id=to_d(k),
            device_id_type=MESH,
        )

    loop(1, n_m, lambda k: part_flow(k).start())
    loop(1, n_m, lambda k: part_flow(k).wait_recv())
    total = parts[...]
    for m in range(n_m):
        total = total + jnp.where(me_m == m, 0.0, got[m])
    each = total[0:1] / jnp.sqrt(total[1:2] / D + EPSILON)
    lane = lax.broadcasted_iota(jnp.int32, (128, 128), 0)
    slot = lax.broadcasted_iota(jnp.int32, (128, 128), 1)
    pick = jnp.where(lane % 16 == slot, 1.0, 0.0)
    score = jnp.dot(
        jnp.broadcast_to(each, (8, 128)),
        pick,
        precision=lax.Precision.HIGHEST,
        preferred_element_type=jnp.float32,
    )[0:1] * (1.0 / 8)
    direct = total[2:3] / jnp.sqrt(total[3:4] / D + EPSILON)
    rerank[...] = direct + score
    shard = lax.broadcasted_iota(jnp.int32, (n_d, 128), 0)
    slots = jnp.where(shard == target[...], score, 0.0)
    rows[...] = slots
    loop(1, n_d, lambda k: score_flow(k).start())
    loop(1, n_d, lambda k: score_flow(k).wait_recv())
    mine = shard == me_d
    channel[...] = jnp.sum(jnp.where(mine, slots, inbox[...]), axis=0, keepdims=True)
    loop(1, n_m, lambda k: part_flow(k).wait_send())
    loop(1, n_d, lambda k: score_flow(k).wait_send())


def scores(parts, target):
    return pl.pallas_call(
        score_kernel,
        out_shape=[jax.ShapeDtypeStruct((1, 128), jnp.float32)] * 2,
        in_specs=[pl.BlockSpec(memory_space=VMEM)] * 2,
        out_specs=[pl.BlockSpec(memory_space=VMEM)] * 2,
        scratch_shapes=[
            pltpu.VMEM((16, 4, 128), jnp.float32),
            pltpu.VMEM((32, 128), jnp.float32),
            pltpu.VMEM((32, 128), jnp.float32),
            pltpu.SemaphoreType.DMA((48,)),
            pltpu.SemaphoreType.DMA((48,)),
        ],
        compiler_params=pltpu.CompilerParams(collective_id=9, has_side_effects=True),
        name="scores",
    )(parts, target)


def folded(weight):
    return jnp.concatenate([weight[:, :128], weight[:, 128:]], axis=0)


def unfolded_dot(rows, weight):
    blocks = weight.reshape(ZL * X, 2, -1, 128)
    halves = [dot(rows, blocks[:, h].reshape(-1, 128)) for h in range(2)]
    return jnp.concatenate(halves, axis=1)


def shards(
    hidden,
    wq_direct,
    wkv_direct,
    wo_direct,
    kv_cache,
    parent,
    lengths,
    cand_embed,
    source,
    enc_qkv,
    enc_out,
    cross_q,
    cross_kv,
    cross_out,
    w_direct,
    w_channel,
    target_shard,
):
    bf16 = jnp.bfloat16
    beam_n, len_n, width = cand_embed.shape
    rows_n = beam_n * len_n
    own_start = lax.axis_index(MP) * width
    rows = jnp.concatenate(
        [cand_embed.reshape(rows_n, width), jnp.tile(source[0], (2, 1))], axis=0
    )
    first_pack = jnp.concatenate([enc_qkv[0], enc_qkv[1], enc_qkv[2], cross_q, folded(enc_out)], 1)
    second_pack = jnp.concatenate([cross_kv[0], cross_kv[1], folded(cross_out)], 1)
    rows_full, first_full, second_full = gather(
        rows, 3, (1, 2, 5, 8, 9, 10), [first_pack[None], second_pack[None]], 1
    )
    query_new = dot(hidden, wq_direct).astype(bf16)
    key_new = dot(hidden, wkv_direct[0]).astype(bf16)
    value_new = dot(hidden, wkv_direct[1]).astype(bf16)
    local = pltpu.VMEM((rows_n, 2 * HD), bf16)
    direct_context = local_call(
        direct_kernel,
        (beam_n, 2 * HD),
        [parent, lengths],
        [query_new, key_new, value_new, kv_cache],
        [local, local],
    )
    enc = dot(rows_full, first_full[0]).astype(bf16)
    enc_context = local_call(encoder_kernel, (rows_n, 2 * HD), [parent, lengths], [enc])
    contexts = jnp.concatenate([enc_context, direct_context], axis=0)
    (context_full,) = gather(contexts, 3, (), [], 2)
    hidden_share = lax.dynamic_slice_in_dim(hidden, own_start, width, 1).astype(jnp.float32)
    new_state = hidden_share + dot(context_full[rows_n : rows_n + beam_n], wo_direct)
    tokens = cand_embed[parent].reshape(rows_n, width)
    summed = tokens.astype(jnp.float32) + unfolded_dot(
        context_full[:rows_n], first_full[0, :, 4 * 2 * HD :]
    )
    cross_queries = enc[rows_n : rows_n + 8, 3 * 2 * HD : 4 * 2 * HD]
    (summed_full,) = gather(summed.astype(bf16), 4, (), [], 3)
    wide = summed_full.astype(jnp.float32)
    norm = jnp.sqrt(jnp.mean(wide * wide, axis=1, keepdims=True) + EPSILON)
    keys_values = (dot(summed_full, second_full[0, :, : 4 * HD]) / norm).astype(bf16)
    cross_context = local_call(
        cross_kernel,
        (8 * beam_n, 2 * HD),
        [lengths],
        [jnp.repeat(cross_queries, beam_n, axis=0), keys_values],
    )
    (cross_context_full,) = gather(cross_context, 1, (), [], 4)
    decoded = unfolded_dot(cross_context_full, second_full[0, :, 4 * HD :])
    decoded = decoded + jnp.repeat(source[0].astype(jnp.float32), beam_n, axis=0)
    lanes = ((0, 128 - beam_n),)
    parts = jnp.stack(
        [
            jnp.sum(decoded * w_channel.astype(jnp.float32), axis=1),
            jnp.sum(decoded * decoded, axis=1),
            jnp.pad(jnp.sum(new_state * w_direct.astype(jnp.float32), axis=1), lanes),
            jnp.pad(jnp.sum(new_state * new_state, axis=1), lanes),
        ]
    )
    target = jnp.pad(target_shard[None], ((0, 0), (0, 128 - beam_n)), constant_values=-1)
    rerank, channel = scores(parts, target)
    return (new_state.astype(bf16), rerank[0, :beam_n], channel[0, :beam_n])


def solution(mesh):
    split = Mesh(mesh.devices.reshape(ZL, X, Y, ZH, C), AX)
    in_specs = (
        P(DP, None),
        P(None, MP),
        P(None, None, MP),
        P(None, MP),
        P(None, DP, None, MP),
        P(DP),
        P(DP),
        P(DP, None, MP),
        P(DP, None, MP),
        P(None, DP, MP),
        P(DP, MP),
        P(DP, MP),
        P(None, DP, MP),
        P(DP, MP),
        P(MP),
        P(MP),
        P(DP),
    )
    out_specs = (P(DP, MP), P(DP), P(DP))
    return jax.shard_map(
        shards, mesh=split, in_specs=in_specs, out_specs=out_specs, check_vma=False
    )
```

time: 322 us -> 266 us (0.83)
  Pallas kernels: 282 us -> 224 us
  local copies, waits for them, and re-layouts: 7.02 us -> 18.7 us
  matrix products: 23.9 us -> 17.2 us
    pallas_call x4, Pallas kernels: 243 us -> 188 us  [gather(): pl.pallas_call(functools.partial(gather_kernel, chunks, plan, n_dp), out_...]
    dot_general x12 -> x10, matrix products: 23.9 us -> 17.2 us  [dot(): return jnp.dot(a, b, preferred_element_type=jnp.float32)]
    slice x0 -> x7, local copies, waits for them, and re-layouts: none -> 4.84 us  [the longest x2 1.48 us: folded(): return jnp.concatenate([weight[:, :128], weight[:, 128:]], axis=0)]
    unnamed x30, local copies, waits for them, and re-layouts: 2.42 us -> 6.51 us
    pallas_call x1, Pallas kernels: 30.1 us -> 26.6 us  [scores(): pl.pallas_call(score_kernel, out_shape=[jax.ShapeDtypeStruct((1, 128), jn...]
where the time goes in v2:
time: 266 us; the launch traced here: 265 us
  Pallas kernels  224 us (84%)
  local copies, waits for them, and re-layouts  18.7 us (7%)
  matrix products  17.2 us (6%)
  other arithmetic  4.48 us (2%)
    pallas_call x4, Pallas kernels, gather(): pl.pallas_call(functools.partial(gather_kernel, chunks, plan, n_dp), out_...  188 us
    pallas_call x1, Pallas kernels, scores(): pl.pallas_call(score_kernel, out_shape=[jax.ShapeDtypeStruct((1, 128), jn...  26.6 us
    dot_general x10, matrix products, dot(): return jnp.dot(a, b, preferred_element_type=jnp.float32)  17.2 us
    pallas_call x3, Pallas kernels, local_call(): pl.pallas_call(kernel, out_shape=jax.ShapeDtypeStruct(out_shape, jnp.bflo...  9.25 us
    unnamed x30, local copies, waits for them, and re-layouts  6.51 us

profile of v2, /device:TPU:1, one launch (start us, length us, event | category | flops | bytes accessed | tf_op | source)
XLA Modules:
  0.0 265.0 jit_solution(3766404763746192707)
XLA Ops:
  0.6 0.9 slice_bitcast_fusion.1
  6.8 1.0 pad_maximum_fusion.refs_0_
  7.8 105.1 %gather_1.1 = (bf16[528,4096]{1,0:T(8,128)(2,1)}, bf16[1,4096,640]{2,1,0:T(8,128)(2,1)}, bf16[1,4096,384]{2,1,0:T(8,128)(2,1)S(1)}) custom-call(bf16[528,256]{1,0:T(8,128)(2,1)S(1)} %pad_maximum_fusion.refs_0_, bf16[1,128,640]{2,1,0:T(8,128)(2,1)S(1)} %bitcast.75, bf16[1,128,384]{2,1,0:T(8,128)(2,1)S(1)} %maximum_bitcast_fusion.refs_2_), custom_call_target="tpu_custom_call" | custom-call | tf_op jit(solution)/shard_map/gather_1/pallas_call | solution.py:292
  112.8 1.7 copy-done.1
  114.5 8.4 %fusion.9.enc = bf16[528,640]{1,0:T(8,128)(2,1)} fusion(bf16[528,4096]{1,0:T(8,128)(2,1)} %get-tuple-element.8, bf16[1,4096,640]{2,1,0:T(8,128)(2,1)} %get-tuple-element.9), kind=kOutput, calls=%fused_computation.11 | convolution fusion | flops 2768578560 | bytes 10244096 | tf_op jit(solution)/shard_map/dot_general | solution.py:310
  122.9 4.5 %shard_map.184 = bf16[512,128]{1,0:T(8,128)(2,1)} custom-call(s32[16]{0:T(128)} %parent.3, s32[16]{0:T(128)} %lengths.5, bf16[528,640]{1,0:T(8,128)(2,1)} %fusion.9.enc), custom_call_target="tpu_custom_call" | custom-call | tf_op jit(solution)/shard_map/pallas_call | solution.py:402
  129.9 2.4 shard_map.185
  132.9 27.2 %gather_2.1 = bf16[528,2048]{1,0:T(8,128)(2,1)S(1)} custom-call(bf16[528,128]{1,0:T(8,128)(2,1)S(1)} %pad_maximum_fusion.1.refs_0_), custom_call_target="tpu_custom_call" | custom-call | tf_op jit(solution)/shard_map/gather_2/pallas_call | solution.py:292
  160.2 1.3 slice.83
  161.5 1.4 fusion.7
  163.0 1.4 fusion.5
  164.4 2.2 gather_fusion
  166.6 1.2 fusion.22.refs_0_
  167.8 33.6 %gather_3.1 = bf16[512,4096]{1,0:T(8,128)(2,1)S(1)} custom-call(bf16[512,256]{1,0:T(8,128)(2,1)S(1)} %fusion.22.refs_0_), custom_call_target="tpu_custom_call" | custom-call | tf_op jit(solution)/shard_map/gather_3/pallas_call | solution.py:292
  201.3 0.9 multiply_reduce_fusion
  202.3 1.0 copy-done.2
  203.2 1.9 fusion.15.kv
  206.4 2.4 shard_map.186.refs_0_
  209.6 22.0 %gather_4.1 = bf16[128,2048]{1,0:T(8,128)(2,1)S(1)} custom-call(bf16[128,128]{1,0:T(8,128)(2,1)S(1)} %copy-done.3), custom_call_target="tpu_custom_call" | custom-call | tf_op jit(solution)/shard_map/gather_4/pallas_call | solution.py:292
  231.6 1.3 slice.87
  233.9 1.0 multiply_reduce_fusion.4
  236.1 26.6 %scores.1 = (f32[1,128]{1,0:T(1,128)}, f32[1,128]{1,0:T(1,128)}) custom-call(f32[4,128]{1,0:T(4,128)} %pad_maximum_fusion.2.parts, s32[1,128]{1,0:T(1,128)} %pad.13.target), custom_call_target="tpu_custom_call" | custom-call | tf_op jit(solution)/shard_map/scores/pallas_call | solution.py:491
  262.7 1.1 slice_bitcast_fusion.2
  263.8 1.2 slice_bitcast_fusion.3
  (55 shorter events, 12.7 us)
Async XLA Ops:
  0.6 233.3 %copy-start = (bf16[2048,256]{1,0:T(8,128)(2,1)S(1)}, bf16[2048,256]{1,0:T(8,128)(2,1)}, u32[]{:S(2)}) copy-start(bf16[2048,256]{1,0:T(8,128)(2,1)} %param.20) | copy-start | bytes 3145732
  112.8 1.7 copy-start.1
  114.5 12.8 %copy-start.4 = (bf16[2,4096,128]{2,1,0:T(8,128)(2,1)S(1)}, bf16[2,4096,128]{2,1,0:T(8,128)(2,1)}, u32[]{:S(2)}) copy-start(bf16[2,4096,128]{2,1,0:T(8,128)(2,1)} %param.19) | copy-start | bytes 6291460
  114.5 12.8 %copy-start.5 = (bf16[16,4096]{1,0:T(8,128)(2,1)S(1)}, bf16[16,4096]{1,0:T(8,128)(2,1)}, u32[]{:S(2)}) copy-start(bf16[16,4096]{1,0:T(8,128)(2,1)} %param.17) | copy-start | bytes 393220
  127.3 1.7 copy-start.6
  127.3 4.9 %copy-start.7 = (bf16[512,128]{1,0:T(8,128)(2,1)S(1)}, bf16[512,128]{1,0:T(8,128)(2,1)}, u32[]{:S(2)}) copy-start(bf16[512,128]{1,0:T(8,128)(2,1)} %shard_map.184) | copy-start | bytes 393220
  163.0 1.4 copy-start.9
  201.3 1.9 copy-start.2
  208.9 0.8 copy-start.3
  232.9 0.7 copy-start.8
  232.9 0.7 copy-start.10
  232.9 1.0 copy-start.11
  233.0 2.5 copy-start.12

commit v3 on v2

--- a/solution.py
+++ b/solution.py
@@ -544,7 +544,7 @@
     first_pack = jnp.concatenate([enc_qkv[0], enc_qkv[1], enc_qkv[2], cross_q, folded(enc_out)], 1)
     second_pack = jnp.concatenate([cross_kv[0], cross_kv[1], folded(cross_out)], 1)
     rows_full, first_full, second_full = gather(
-        rows, 3, (1, 2, 5, 8, 9, 10), [first_pack[None], second_pack[None]], 1
+        rows, 3, (1, 2, 4, 9, 10, 11), [first_pack[None], second_pack[None]], 1
     )
     query_new = dot(hidden, wq_direct).astype(bf16)
     key_new = dot(hidden, wkv_direct[0]).astype(bf16)

time: 266 us -> 266 us (level)
  no operation moved by 1% of the time
where the time goes in v3:
time: 266 us; the launch traced here: 265 us
  Pallas kernels  223 us (84%)
  local copies, waits for them, and re-layouts  18.7 us (7%)
  matrix products  17.2 us (6%)
  other arithmetic  4.48 us (2%)
    pallas_call x4, Pallas kernels, gather(): pl.pallas_call(functools.partial(gather_kernel, chunks, plan, n_dp), out_...  188 us
    pallas_call x1, Pallas kernels, scores(): pl.pallas_call(score_kernel, out_shape=[jax.ShapeDtypeStruct((1, 128), jn...  26.1 us
    dot_general x10, matrix products, dot(): return jnp.dot(a, b, preferred_element_type=jnp.float32)  17.2 us
    pallas_call x3, Pallas kernels, local_call(): pl.pallas_call(kernel, out_shape=jax.ShapeDtypeStruct(out_shape, jnp.bflo...  9.24 us
    unnamed x30, local copies, waits for them, and re-layouts  6.51 us

profile of v3, /device:TPU:1, one launch (start us, length us, event | category | flops | bytes accessed | tf_op | source)
XLA Modules:
  0.0 264.8 jit_solution(8571223659742053634)
XLA Ops:
  0.6 0.9 slice_bitcast_fusion.1
  6.8 1.0 pad_maximum_fusion.refs_0_
  7.8 107.8 %gather_1.1 = (bf16[528,4096]{1,0:T(8,128)(2,1)}, bf16[1,4096,640]{2,1,0:T(8,128)(2,1)}, bf16[1,4096,384]{2,1,0:T(8,128)(2,1)S(1)}) custom-call(bf16[528,256]{1,0:T(8,128)(2,1)S(1)} %pad_maximum_fusion.refs_0_, bf16[1,128,640]{2,1,0:T(8,128)(2,1)S(1)} %bitcast.75, bf16[1,128,384]{2,1,0:T(8,128)(2,1)S(1)} %maximum_bitcast_fusion.refs_2_), custom_call_target="tpu_custom_call" | custom-call | tf_op jit(solution)/shard_map/gather_1/pallas_call | solution.py:292
  115.6 1.7 copy-done.1
  117.3 8.4 %fusion.9.enc = bf16[528,640]{1,0:T(8,128)(2,1)} fusion(bf16[528,4096]{1,0:T(8,128)(2,1)} %get-tuple-element.8, bf16[1,4096,640]{2,1,0:T(8,128)(2,1)} %get-tuple-element.9), kind=kOutput, calls=%fused_computation.11 | convolution fusion | flops 2768578560 | bytes 10244096 | tf_op jit(solution)/shard_map/dot_general | solution.py:310
  125.6 4.5 %shard_map.184 = bf16[512,128]{1,0:T(8,128)(2,1)} custom-call(s32[16]{0:T(128)} %parent.3, s32[16]{0:T(128)} %lengths.5, bf16[528,640]{1,0:T(8,128)(2,1)} %fusion.9.enc), custom_call_target="tpu_custom_call" | custom-call | tf_op jit(solution)/shard_map/pallas_call | solution.py:402
  132.6 2.4 shard_map.185
  135.7 27.3 %gather_2.1 = bf16[528,2048]{1,0:T(8,128)(2,1)S(1)} custom-call(bf16[528,128]{1,0:T(8,128)(2,1)S(1)} %pad_maximum_fusion.1.refs_0_), custom_call_target="tpu_custom_call" | custom-call | tf_op jit(solution)/shard_map/gather_2/pallas_call | solution.py:292
  163.0 1.3 slice.83
  164.4 1.4 fusion.7
  165.8 1.4 fusion.5
  167.2 2.2 gather_fusion
  169.4 1.2 fusion.22.refs_0_
  170.6 32.1 %gather_3.1 = bf16[512,4096]{1,0:T(8,128)(2,1)S(1)} custom-call(bf16[512,256]{1,0:T(8,128)(2,1)S(1)} %fusion.22.refs_0_), custom_call_target="tpu_custom_call" | custom-call | tf_op jit(solution)/shard_map/gather_3/pallas_call | solution.py:292
  202.7 0.9 multiply_reduce_fusion
  203.6 1.0 copy-done.2
  204.6 1.9 fusion.15.kv
  207.8 2.4 shard_map.186.refs_0_
  211.0 20.9 %gather_4.1 = bf16[128,2048]{1,0:T(8,128)(2,1)S(1)} custom-call(bf16[128,128]{1,0:T(8,128)(2,1)S(1)} %copy-done.3), custom_call_target="tpu_custom_call" | custom-call | tf_op jit(solution)/shard_map/gather_4/pallas_call | solution.py:292
  231.9 1.3 slice.87
  234.3 1.0 multiply_reduce_fusion.4
  236.4 26.1 %scores.1 = (f32[1,128]{1,0:T(1,128)}, f32[1,128]{1,0:T(1,128)}) custom-call(f32[4,128]{1,0:T(4,128)} %pad_maximum_fusion.2.parts, s32[1,128]{1,0:T(1,128)} %pad.13.target), custom_call_target="tpu_custom_call" | custom-call | tf_op jit(solution)/shard_map/scores/pallas_call | solution.py:491
  262.5 1.1 slice_bitcast_fusion.2
  263.6 1.2 slice_bitcast_fusion.3
  (55 shorter events, 12.7 us)
Async XLA Ops:
  0.6 233.6 %copy-start = (bf16[2048,256]{1,0:T(8,128)(2,1)S(1)}, bf16[2048,256]{1,0:T(8,128)(2,1)}, u32[]{:S(2)}) copy-start(bf16[2048,256]{1,0:T(8,128)(2,1)} %param.20) | copy-start | bytes 3145732
  115.6 1.7 copy-start.1
  117.3 12.8 %copy-start.4 = (bf16[2,4096,128]{2,1,0:T(8,128)(2,1)S(1)}, bf16[2,4096,128]{2,1,0:T(8,128)(2,1)}, u32[]{:S(2)}) copy-start(bf16[2,4096,128]{2,1,0:T(8,128)(2,1)} %param.19) | copy-start | bytes 6291460
  117.3 12.8 %copy-start.5 = (bf16[16,4096]{1,0:T(8,128)(2,1)S(1)}, bf16[16,4096]{1,0:T(8,128)(2,1)}, u32[]{:S(2)}) copy-start(bf16[16,4096]{1,0:T(8,128)(2,1)} %param.17) | copy-start | bytes 393220
  130.1 1.7 copy-start.6
  130.1 4.9 %copy-start.7 = (bf16[512,128]{1,0:T(8,128)(2,1)S(1)}, bf16[512,128]{1,0:T(8,128)(2,1)}, u32[]{:S(2)}) copy-start(bf16[512,128]{1,0:T(8,128)(2,1)} %shard_map.184) | copy-start | bytes 393220
  165.8 1.4 copy-start.9
  202.7 1.9 copy-start.2
  210.2 0.8 copy-start.3
  233.2 0.7 copy-start.8
  233.2 0.7 copy-start.10
  233.2 1.0 copy-start.11
  233.3 2.5 copy-start.12
